TPU v7x, 256 devices: a whole 4x4x8 slice. The times are simulated.
256 devices in a mesh: ctx: 128 (over x, y, z), tp: 2 (over core).
Axes of the slice: x: 4, y: 4, z: 8, core: 2. Of those that a mesh axis runs over, the one named last changes fastest.
Arguments:
- queries: bfloat16 [8192, 2560], P('ctx', 'tp'), may hold values from -100 to 100
- projected_keys: bfloat16 [8192, 512], P('ctx', 'tp'), may hold values from -30 to 30
- projected_values: bfloat16 [8192, 512], P('ctx', 'tp'), may hold values from -6 to 6
- hidden: bfloat16 [8192, 5120], P('ctx', 'tp'), may hold values from -6 to 6
- route_ids: int32 [8192, 1], P('ctx'), may hold values from 0 to 15; in each aligned block of 64 rows (0 to 63, 64 to 127, ...) at most 6 rows name the same one
- route_gain: float32 [8192], P('ctx'), may hold values from 0.25 to 1
- w_gate: bfloat16 [128, 5120, 512], P('ctx', None, 'tp'), may hold values from -0.078125 to 0.078125
- w_up: bfloat16 [128, 5120, 512], P('ctx', None, 'tp'), may hold values from -0.078125 to 0.078125
- w_down: bfloat16 [128, 512, 5120], P('ctx', None, 'tp'), may hold values from -0.09375 to 0.09375
Outputs:
- attended: bfloat16 [8192, 2560], P('ctx', 'tp')
- mixed: bfloat16 [8192, 5120], P('ctx', 'tp')
Inputs may be any that keep to these rules, and one draw needn't show every extreme that they name: `route_ids`: within the rows of one device (aligned blocks of 64 rows) no expert is named more than 6 times, a bound that some block reaches.
All inputs are finite; a program needn't handle non-finite values.
Results may differ from a plain program's by a relative error of at most 0.0057.
Values may be sent and summed in bfloat16 or wider, within the bound.
A program may use at most 128 MiB of HBM per device.

v0:
```python
import math

import jax
import jax.numpy as jnp
from jax import lax
from jax.sharding import PartitionSpec as P

HEAD_SIZE = 128
EXPERTS = 16
CAP = 6


masked_score = -1e30


def sent_together(arrays, axis, dim, along):
    widths = [a.shape[along] for a in arrays]
    both = jnp.concatenate(arrays, axis=along)
    result = lax.all_gather(both, axis, axis=dim, tiled=True)
    return tuple(jnp.split(result, [sum(widths[:k]) for k in range(1, len(widths))], axis=along))


def joined_along(parts, dim):
    dims = list(parts.shape[1:])
    dims[dim] *= parts.shape[0]
    return jnp.moveaxis(parts, 0, dim).reshape(dims)


def copy_for_each(value, axis):
    count = lax.axis_size(axis)
    return lax.all_to_all(
        jnp.broadcast_to(value[None], (count, *value.shape)), axis, 0, 0, tiled=True
    )


def gathered_copies(value, axis, dim):
    return joined_along(copy_for_each(value, axis), dim)


def cut_along(value, dim, count):
    dims = value.shape
    parts = value.reshape(*dims[:dim], count, dims[dim] // count, *dims[dim + 1 :])
    return jnp.moveaxis(parts, dim, 0)


def piece_ends(length, count):
    hop = length // count
    if hop >= 8:
        hop -= hop % 8
    return [hop * k for k in range(1, count)]


def exchange_in_pieces(value, axis, pieces, split_dim, concat_dim):
    parts = cut_along(value, split_dim, lax.axis_size(axis))
    cut = max(range(1, max(2, parts.ndim - 1)), key=lambda d: parts.shape[d])
    gathered = []
    for section in jnp.split(parts, piece_ends(parts.shape[cut], pieces), axis=cut):
        if section.size:
            gathered.append(lax.all_to_all(section, axis, split_axis=0, concat_axis=0, tiled=True))
    return joined_along(jnp.concatenate(gathered, axis=cut), concat_dim)


def body(
    queries, projected_keys, projected_values, hidden, route_ids, route_gain, w_gate, w_up, w_down
):
    tok_rows = queries.shape[0]
    width_q = queries.shape[1]
    width_kv = projected_keys.shape[1]
    ctx_count = lax.axis_size("ctx")
    ctx_index = lax.axis_index("ctx")
    offsets = jnp.arange(tok_rows, dtype=jnp.int32)
    query_use, key_use, value_use = (queries, projected_keys, projected_values)

    def position(device, offset):
        return device * tok_rows + offset

    query_pos = position(ctx_index, offsets)
    query_top = jnp.max(query_pos)
    kv_heads = width_kv // HEAD_SIZE
    head_group = width_q // HEAD_SIZE // kv_heads
    query_tensor = query_use.reshape(tok_rows, kv_heads, head_group, HEAD_SIZE)
    score_scale = HEAD_SIZE ** (-0.5)
    key_whole, value_whole = sent_together((key_use, value_use), "ctx", 0, 1)
    total_rows = key_whole.shape[0]
    block_rows = math.gcd(total_rows, 1024)

    def absorb_block(block_index, state):
        block_start = block_index * block_rows
        key_block = lax.dynamic_slice_in_dim(key_whole, block_start, block_rows, 0).reshape(
            block_rows, kv_heads, HEAD_SIZE
        )
        value_block = lax.dynamic_slice_in_dim(value_whole, block_start, block_rows, 0).reshape(
            block_rows, kv_heads, HEAD_SIZE
        )
        global_rows = block_start + jnp.arange(block_rows, dtype=jnp.int32)
        key_pos = position(global_rows // tok_rows, global_rows % tok_rows)

        def update(inner_state):
            running_max, running_sum, running_out = inner_state
            scores = (
                jnp.einsum(
                    "qhgd,khd->hgqk", query_tensor, key_block, preferred_element_type=jnp.float32
                )
                * score_scale
            )
            allowed = query_pos[:, None] >= key_pos[None, :]
            scores = jnp.where(allowed, scores, masked_score)
            new_max = jnp.maximum(running_max, jnp.max(scores, axis=3))
            weights = jnp.where(allowed, jnp.exp(scores - new_max[..., None]), 0.0)
            factor = jnp.exp(running_max - new_max)
            new_sum = running_sum * factor + jnp.sum(weights, axis=3)
            partial_out = jnp.einsum(
                "hgqk,khd->qhgd",
                weights.astype(jnp.bfloat16),
                value_block,
                preferred_element_type=jnp.float32,
            )
            new_out = running_out * jnp.transpose(factor, (2, 0, 1))[..., None] + partial_out
            return (new_max, new_sum, new_out)

        def keep_state(inner_state):
            return inner_state

        return lax.cond(jnp.min(key_pos) <= query_top, update, keep_state, state)

    initial = (
        jnp.full((kv_heads, head_group, tok_rows), masked_score, jnp.float32),
        jnp.zeros((kv_heads, head_group, tok_rows), jnp.float32),
        jnp.zeros((tok_rows, kv_heads, head_group, HEAD_SIZE), jnp.float32),
    )
    running_max, running_sum, running_out = lax.fori_loop(
        0, total_rows // block_rows, absorb_block, initial
    )
    attended = (
        (running_out / jnp.transpose(running_sum, (2, 0, 1))[..., None])
        .reshape(tok_rows, width_q)
        .astype(jnp.bfloat16)
    )
    ids_flat = route_ids[:, 0]
    chosen = (ids_flat[:, None] == jnp.arange(EXPERTS, dtype=jnp.int32)[None, :]).astype(jnp.int32)
    ranking = jnp.sum((jnp.cumsum(chosen, axis=0) - chosen) * chosen, axis=1)
    slot_of = ids_flat * CAP + ranking
    selector = (jnp.arange(EXPERTS * CAP, dtype=jnp.int32)[:, None] == slot_of[None, :]).astype(
        jnp.bfloat16
    )
    host_count = ctx_count // EXPERTS
    feature_width = hidden.shape[1]
    packed = jnp.dot(selector, hidden, preferred_element_type=jnp.float32).astype(jnp.bfloat16)
    packed = jnp.broadcast_to(
        packed.reshape(EXPERTS, 1, CAP, feature_width), (EXPERTS, host_count, CAP, feature_width)
    ).reshape(ctx_count, CAP, feature_width)
    arrived = lax.all_to_all(packed, "ctx", split_axis=0, concat_axis=0, tiled=True)
    arrived = lax.all_gather(arrived, "tp", axis=2, tiled=True)
    slot_count = arrived.shape[1]
    flat_rows = arrived.reshape(-1, arrived.shape[2])
    gate_val = jnp.dot(flat_rows, w_gate[0], preferred_element_type=jnp.float32)
    up_val = jnp.dot(flat_rows, w_up[0], preferred_element_type=jnp.float32)
    inner = (jax.nn.silu(gate_val) * up_val).astype(jnp.bfloat16)
    pair_inner = gathered_copies(inner, "tp", 1)
    partial_out = jnp.dot(pair_inner, w_down[0], preferred_element_type=jnp.float32).astype(
        jnp.bfloat16
    )
    partial_out = partial_out.reshape(ctx_count, slot_count, partial_out.shape[1])
    returned = exchange_in_pieces(partial_out, "ctx", 2, 0, 0)
    out_width = returned.shape[2]
    summed = returned.reshape(EXPERTS, host_count, CAP, out_width).astype(jnp.float32).sum(axis=1)
    summed = summed.reshape(EXPERTS * CAP, out_width)
    mixed = (summed[slot_of] * route_gain[:, None]).astype(jnp.bfloat16)
    return (attended, mixed)


def solution(mesh):
    in_specs = (
        P("ctx", "tp"),
        P("ctx", "tp"),
        P("ctx", "tp"),
        P("ctx", "tp"),
        P("ctx", None),
        P("ctx"),
        P("ctx", None, "tp"),
        P("ctx", None, "tp"),
        P("ctx", None, "tp"),
    )
    out_specs = (P("ctx", "tp"), P("ctx", "tp"))
    return jax.shard_map(body, mesh=mesh, in_specs=in_specs, out_specs=out_specs, check_vma=False)
```

profile of v0, /device:TPU:30, one launch (start us, length us, event | category | flops | bytes accessed | tf_op | source)
XLA Modules:
  0.0 413.4 jit_solution(2992642349980450384)
XLA Ops:
  7.2 0.9 fusion.37
  9.7 2.0 convolution_convert_fusion.1
  11.7 1.2 broadcast_in_dim.56
  13.3 133.1 %all_to_all.20 = bf16[128,6,2560]{2,1,0:T(8,128)(2,1)} all-to-all(bf16[128,6,2560]{2,1,0:T(8,128)(2,1)S(1)} %bitcast.74), channel_id=1, replica_groups=mesh['ctx'=128,'tp'=2] {'ctx'}, dimensions={0} | all-to-all | bytes 7864320 | tf_op jit(solution)/shard_map/all_to_all | solution.py:152
  147.8 23.5 %all-gather.5.cloned.1.call-done = bf16[128,6,5120]{2,1,0:T(8,128)(2,1)} async-done(((bf16[128,6,2560]{2,1,0:T(8,128)(2,1)}), bf16[128,6,5120]{2,1,0:T(8,128)(2,1)}) %all-gather.5.cloned.1.call-update) | async-done | bytes 7864336 | tf_op jit(solution)/shard_map/all_gather | solution.py:153
  171.3 13.2 %reshape.67 = bf16[768,5120]{1,0:T(8,128)(2,1)} reshape(bf16[128,6,5120]{2,1,0:T(8,128)(2,1)} %all-gather.5.cloned.1.call-done) | data formatting | bytes 15728640 | tf_op jit(solution)/shard_map/reshape | solution.py:155
  184.5 6.3 %fusion.29 = f32[768,256]{1,0:T(8,128)S(1)} fusion(bf16[768,5120]{1,0:T(8,128)(2,1)} %reshape.67, bf16[1,5120,256]{2,1,0:T(8,128)(2,1)} %param.19), kind=kOutput, calls=%fused_computation.45 | convolution fusion | flops 2013265920 | bytes 11272192 | tf_op jit(solution)/shard_map/dot_general | solution.py:156
  191.5 2.2 fusion.34
  194.0 4.4 %all_to_all.21 = bf16[2,768,256]{1,2,0:T(8,128)(2,1)S(1)} all-to-all(bf16[2,768,256]{1,2,0:T(8,128)(2,1)S(1)} %broadcast_in_dim.58), channel_id=1, replica_groups=mesh['ctx'=128,'tp'=2] {'tp'}, dimensions={0} | all-to-all | bytes 1572864 | tf_op jit(solution)/shard_map/all_to_all | solution.py:31
  198.3 4.1 convolution_convert_fusion
  202.5 7.1 %reshape_reshape.4 = bf16[128,1,6,2560]{3,2,0,1:T(8,128)(2,1)} reshape(bf16[768,2560]{1,0:T(8,128)(2,1)} %convolution_convert_fusion) | data formatting | bytes 7864320 | tf_op jit(solution)/shard_map/reshape;reshape | solution.py:42
  209.6 7.9 %slice_bitcast_fusion.1 = (bf16[128,1,3,2560]{3,2,1,0:T(4,128)(2,1)S(1)}, bf16[128,1,3,2560]{3,2,1,0:T(4,128)(2,1)}) fusion(bf16[128,1,6,2560]{3,2,0,1:T(8,128)(2,1)} %reshape_reshape.4), kind=kLoop, calls=%fused_computation.41 | loop fusion | bytes 7864320 | tf_op jit(solution)/shard_map/split | solution.py:57
  217.5 92.6 %all_to_all.22 = bf16[128,1,3,2560]{3,2,1,0:T(4,128)(2,1)} all-to-all(bf16[128,1,3,2560]{3,2,1,0:T(4,128)(2,1)S(1)} %get-tuple-element.430), channel_id=1, replica_groups=mesh['ctx'=128,'tp'=2] {'ctx'}, dimensions={0} | all-to-all | bytes 3932160 | tf_op jit(solution)/shard_map/all_to_all | solution.py:59
  310.1 11.6 %all-to-all-start.3 = ((bf16[128,1,3,2560]{3,2,1,0:T(4,128)(2,1)}), bf16[128,1,3,2560]{3,2,1,0:T(4,128)(2,1)}, u32[]{:S(2)}, u32[]{:S(2)}) async-start(bf16[128,1,3,2560]{3,2,1,0:T(4,128)(2,1)} %get-tuple-element.431), calls=%async_computation.3 | async-start | bytes 5242880 | tf_op jit(solution)/shard_map/all_to_all | solution.py:59
  322.7 4.8 %all-gather.3.cloned.1.call-done = bf16[8192,512]{1,0:T(8,128)(2,1)} async-done(((bf16[64,512]{1,0:T(8,128)(2,1)}), bf16[8192,512]{1,0:T(8,128)(2,1)}) %all-gather.3.cloned.1.call-update) | async-done | bytes 8388624 | tf_op jit(solution)/shard_map/all_gather | solution.py:19
  327.5 5.7 %fusion.40 = (bf16[8192,256]{1,0:T(8,128)(2,1)}, bf16[8192,256]{1,0:T(8,128)(2,1)}) fusion(bf16[8192,512]{1,0:T(8,128)(2,1)} %all-gather.3.cloned.1.call-done), kind=kLoop, calls=%fused_computation.63 | loop fusion | bytes 16777216 | tf_op jit(solution)/shard_map/split | solution.py:20
  333.2 6.4 %copy.21 = bf16[8192,256]{0,1:T(8,128)(2,1)} copy(bf16[8192,256]{1,0:T(8,128)(2,1)} %get-tuple-element.429) | data formatting | bytes 8388608
  339.6 6.3 %copy.23 = bf16[8192,256]{0,1:T(8,128)(2,1)} copy(bf16[8192,256]{1,0:T(8,128)(2,1)} %get-tuple-element.428) | data formatting | bytes 8388608
  346.0 46.5 %while.20 = (s32[]{:T(128)}, f32[2,5,64]{2,1,0:T(8,128)S(1)}, f32[2,5,64]{2,1,0:T(8,128)S(1)}, f32[64,2,5,128]{3,0,2,1:T(8,128)S(1)}, s32[]{:T(128)}, /*index=5*...) while((s32[]{:T(128)}, f32[2,5,64]{2,1,0:T(8,128)S(1)}, ...), condition=%wide.region_7.8_spmd.clone, body=%wide.region_1.7_spmd.clone.sunk | while | flops 344318912 | bytes 12141889 | solution.py:131
  348.0 3.8 conditional.3
  348.0 1.3 constant_dynamic-slice_fusion
  350.0 0.9 fusion.11
  353.8 3.8 conditional.3
  353.8 1.3 constant_dynamic-slice_fusion
  355.9 0.9 fusion.11
  359.6 3.8 conditional.3
  359.6 1.3 constant_dynamic-slice_fusion
  361.7 0.9 fusion.11
  365.4 3.8 conditional.3
  365.4 1.3 constant_dynamic-slice_fusion
  367.5 0.9 fusion.11
  371.2 3.8 conditional.3
  371.3 1.3 constant_dynamic-slice_fusion
  373.3 0.9 fusion.11
  377.1 3.8 conditional.3
  377.1 1.3 constant_dynamic-slice_fusion
  379.1 0.9 fusion.11
  382.9 3.8 conditional.3
  382.9 1.3 constant_dynamic-slice_fusion
  384.9 0.9 fusion.11
  388.7 3.8 conditional.3
  388.7 1.3 constant_dynamic-slice_fusion
  390.8 0.9 fusion.11
  392.8 0.9 convert_element_type.49
  393.7 5.1 %pad_maximum_fusion = bf16[128,1,6,2560]{3,2,1,0:T(8,128)(2,1)S(1)} fusion(bf16[128,1,3,2560]{3,2,1,0:T(4,128)(2,1)} %all-to-all-done.3, bf16[128,1,3,2560]{3,2,1,0:T(4,128)(2,1)} %all_to_all.22), kind=kLoop, calls=%fused_computation.37 | loop fusion | flops 7864320 | bytes 7864320 | tf_op jit(solution)/shard_map/concatenate | solution.py:60
  398.7 2.1 convert_reduce_fusion
  400.9 2.6 reshape.69
  403.4 2.3 gather_fusion
  (113 shorter events, 24.6 us)
Async XLA Ops:
  7.2 191.2 %copy-start = (bf16[1,512,2560]{2,1,0:T(8,128)(2,1)S(1)}, bf16[1,512,2560]{2,1,0:T(8,128)(2,1)}, u32[]{:S(2)}) copy-start(bf16[1,512,2560]{2,1,0:T(8,128)(2,1)} %param.21) | copy-start | bytes 7864324
  7.2 164.1 %all-gather.5.cloned.1.call-start = ((), (), s32[]{:S(2)}) async-start(), calls=%async_computation.5 | async-start | bytes 15728640 | tf_op jit(solution)/shard_map/all_gather | solution.py:153
  146.4 0.8 copy-start.4
  146.4 0.8 copy-start.5
  146.4 181.1 %all-gather.3.cloned.1.call-start = ((), (), s32[]{:S(2)}) async-start(), calls=%async_computation.4 | async-start | bytes 8454144 | tf_op jit(solution)/shard_map/all_gather | solution.py:19
  184.5 6.3 %copy-start.2 = (bf16[768,5120]{1,0:T(8,128)(2,1)S(1)}, bf16[768,5120]{1,0:T(8,128)(2,1)}, u32[]{:S(2)}) copy-start(bf16[768,5120]{1,0:T(8,128)(2,1)} %reshape.67) | copy-start | bytes 23592964
  184.5 7.0 %copy-start.8 = (bf16[1,5120,256]{2,1,0:T(8,128)(2,1)S(1)}, bf16[1,5120,256]{2,1,0:T(8,128)(2,1)}, u32[]{:S(2)}) copy-start(bf16[1,5120,256]{2,1,0:T(8,128)(2,1)} %param.20) | copy-start | bytes 7864324
  310.1 12.3 %copy-start.3 = (bf16[64,1280]{1,0:T(8,128)(2,1)S(1)}, bf16[64,1280]{1,0:T(8,128)(2,1)}, u32[]{:S(2)}) copy-start(bf16[64,1280]{1,0:T(8,128)(2,1)} %param.13) | copy-start | bytes 491524
  310.1 12.5 %copy-start.6 = (s32[64,1]{0,1:T(1,128)S(1)}, s32[64,1]{0,1:T(1,128)}, u32[]{:S(2)}) copy-start(s32[64,1]{0,1:T(1,128)} %param.17) | copy-start | bytes 772
  310.1 83.6 %all-to-all-start.3 = ((bf16[128,1,3,2560]{3,2,1,0:T(4,128)(2,1)}), bf16[128,1,3,2560]{3,2,1,0:T(4,128)(2,1)}, u32[]{:S(2)}, u32[]{:S(2)}) async-start(bf16[128,1,3,2560]{3,2,1,0:T(4,128)(2,1)} %get-tuple-element.431), calls=%async_computation.3 | async-start | bytes 5242880 | tf_op jit(solution)/shard_map/all_to_all | solution.py:59
  400.8 5.7 %copy-start.1 = (bf16[1,512,2560]{2,1,0:T(8,128)(2,1)S(1)}, bf16[1,512,2560]{2,1,0:T(8,128)(2,1)}, u32[]{:S(2)}) copy-start(bf16[1,512,2560]{2,1,0:T(8,128)(2,1)} %param.21) | copy-start | bytes 7864324
  403.4 2.3 copy-start.7
Sparse Core Ops, SparseCore 0:
  146.5 24.7 all-gather.4
  175.5 151.9 all-gather.2
where the time goes:
time: 415 us; the launch traced here: 413 us
  blocking collectives  230 us (55%)
  local copies, waits for them, and re-layouts  66.2 us (16%)
  waiting for transfers between devices  28.3 us (7%)
  matrix products  26.9 us (6%)
  other arithmetic  25 us (6%)
  between operations  14.2 us (3%)
  starting transfers between devices  11.6 us (3%)
  loops' own time  11.1 us (3%)
    all_to_all x1, blocking collectives, body(): lax.all_to_all(packed, 'ctx', split_axis=0, concat_axis=0, tiled=True)  133 us
    all_to_all x1, blocking collectives, exchange_in_pieces(): lax.all_to_all(section, axis, split_axis=0, concat_axis=0, tiled=True)  92.6 us
    all_gather x1, waiting for transfers between devices, body(): arrived = lax.all_gather(arrived, 'tp', axis=2, tiled=True)  23.5 us
    unnamed x21, local copies, waits for them, and re-layouts  14.2 us
    reshape x1, local copies, waits for them, and re-layouts, body(): flat_rows = arrived.reshape(-1, arrived.shape[2])  13.2 us
    all_to_all x1, starting transfers between devices, exchange_in_pieces(): lax.all_to_all(section, axis, split_axis=0, concat_axis=0, tiled=True)  11.6 us
    another operation x1, loops' own time, body(): lax.fori_loop(0, total_rows // block_rows, absorb_block, initial)  10.5 us
    dynamic_slice x8, local copies, waits for them, and re-layouts, absorb_block(): lax.dynamic_slice_in_dim(value_whole, block_start, block_rows, 0)  10.2 us
  transfers between devices with their start and end apart: 3, of which 2 were waited for; matrix products, arithmetic and copies ran while one was open for 24% of the time, Pallas kernels for 0%

commit v1 on v0

v1 whole, which is shorter than its diff:
```python
import functools

import jax
import jax.numpy as jnp
from jax import lax
from jax.experimental import pallas as pl
from jax.experimental.pallas import tpu as pltpu
from jax.sharding import PartitionSpec as P

HEAD_SIZE = 128
EXPERTS = 16
CAP = 6
KEY_BLOCK = 512
LOG2E = 1.4426950408889634
NEG = -1e30


def attention_kernel(rows, groups, heads, q_ref, kv_ref, o_ref, kv_buf, m_ref, l_ref, acc_ref, sems):
    me = lax.axis_index("ctx")
    width = groups * HEAD_SIZE
    first = me * rows
    full = first // KEY_BLOCK
    count = full + 1

    def copy(b):
        span = pl.ds(pl.multiple_of(b * KEY_BLOCK, KEY_BLOCK), KEY_BLOCK)
        return pltpu.make_async_copy(kv_ref.at[span], kv_buf.at[span], sems.at[b])

    @pl.loop(0, count)
    def _(b):
        copy(b).start()

    m_ref[...] = jnp.full_like(m_ref, NEG)
    l_ref[...] = jnp.zeros_like(l_ref)
    acc_ref[...] = jnp.zeros_like(acc_ref)
    scale = HEAD_SIZE ** (-0.5) * LOG2E

    def block(b, masked):
        copy(b).wait()
        span = pl.ds(pl.multiple_of(b * KEY_BLOCK, KEY_BLOCK), KEY_BLOCK)
        for g in range(groups):
            k = kv_buf[span, g * HEAD_SIZE : (g + 1) * HEAD_SIZE]
            v = kv_buf[span, width + g * HEAD_SIZE : width + (g + 1) * HEAD_SIZE]
            for h in range(heads):
                i = g * heads + h
                q = q_ref[:, i * HEAD_SIZE : (i + 1) * HEAD_SIZE]
                s = lax.dot_general(q, k, (((1,), (1,)), ((), ())), preferred_element_type=jnp.float32) * scale
                if masked:
                    row = first + lax.broadcasted_iota(jnp.int32, s.shape, 0)
                    col = b * KEY_BLOCK + lax.broadcasted_iota(jnp.int32, s.shape, 1)
                    s = jnp.where(row >= col, s, NEG)
                m_old = m_ref[i]
                m_new = jnp.maximum(m_old, jnp.max(s, axis=1, keepdims=True))
                p = jnp.exp2(s - m_new[:, :1])
                f = jnp.exp2(m_old - m_new)
                l_ref[i] = l_ref[i] * f + jnp.sum(p, axis=1, keepdims=True)
                acc_ref[i] = acc_ref[i] * f + jnp.dot(p.astype(jnp.bfloat16), v, preferred_element_type=jnp.float32)
                m_ref[i] = m_new

    @pl.loop(0, full)
    def _(b):
        block(b, False)

    block(full, True)
    for i in range(groups * heads):
        o_ref[:, i * HEAD_SIZE : (i + 1) * HEAD_SIZE] = (acc_ref[i] / l_ref[i]).astype(jnp.bfloat16)


def attention(queries, kv_whole):
    rows, width_q = queries.shape
    total, width_kv = kv_whole.shape
    groups = width_kv // 2 // HEAD_SIZE
    q_heads = width_q // HEAD_SIZE
    return pl.pallas_call(
        functools.partial(attention_kernel, rows, groups, q_heads // groups),
        name="attention",
        out_shape=jax.ShapeDtypeStruct((rows, width_q), jnp.bfloat16),
        in_specs=[pl.BlockSpec(memory_space=pltpu.VMEM), pl.BlockSpec(memory_space=pl.ANY)],
        out_specs=pl.BlockSpec(memory_space=pltpu.VMEM),
        scratch_shapes=[
            pltpu.VMEM((total, width_kv), jnp.bfloat16),
            pltpu.VMEM((q_heads, rows, HEAD_SIZE), jnp.float32),
            pltpu.VMEM((q_heads, rows, HEAD_SIZE), jnp.float32),
            pltpu.VMEM((q_heads, rows, HEAD_SIZE), jnp.float32),
            pltpu.SemaphoreType.DMA((total // KEY_BLOCK,)),
        ],
        compiler_params=pltpu.CompilerParams(vmem_limit_bytes=40 * 1024 * 1024),
        cost_estimate=pl.CostEstimate(flops=2 * 2 * rows * width_q * total, bytes_accessed=2 * total * width_kv, transcendentals=0),
    )(queries, kv_whole)


def body(queries, projected_keys, projected_values, hidden, route_ids, route_gain, w_gate, w_up, w_down):
    ctx_count = lax.axis_size("ctx")
    hosts = ctx_count // EXPERTS
    half = hidden.shape[1]
    plane = [[e * hosts + z for e in range(EXPERTS)] for z in range(hosts)]
    column = [[e * hosts + z for z in range(hosts)] for e in range(EXPERTS)]

    kv_whole = lax.all_gather(jnp.concatenate([projected_keys, projected_values], axis=1), "ctx", axis=0, tiled=True)

    ids = route_ids[:, 0]
    chosen = (ids[:, None] == jnp.arange(EXPERTS, dtype=jnp.int32)[None, :]).astype(jnp.int32)
    ranking = jnp.sum((jnp.cumsum(chosen, axis=0) - chosen) * chosen, axis=1)
    slot_of = ids * CAP + ranking
    selector = (jnp.arange(EXPERTS * CAP, dtype=jnp.int32)[:, None] == slot_of[None, :]).astype(jnp.bfloat16)
    packed = jnp.dot(selector, hidden, preferred_element_type=jnp.float32).astype(jnp.bfloat16)
    packed = packed.reshape(EXPERTS, CAP, half)
    arrived = lax.all_to_all(packed, "ctx", 0, 0, axis_index_groups=plane, tiled=True)
    arrived = arrived.reshape(EXPERTS * CAP, half)
    rows = lax.all_gather(arrived, "ctx", axis=0, axis_index_groups=column, tiled=True)
    rows = lax.all_gather(rows, "tp", axis=1, tiled=True)
    gate = jnp.dot(rows, w_gate[0], preferred_element_type=jnp.float32)
    up = jnp.dot(rows, w_up[0], preferred_element_type=jnp.float32)
    inner = (jax.nn.silu(gate) * up).astype(jnp.bfloat16)
    inner = lax.all_gather(inner, "tp", axis=1, tiled=True)
    part = jnp.dot(inner, w_down[0], preferred_element_type=jnp.float32).astype(jnp.bfloat16)
    total = lax.psum_scatter(part, "ctx", scatter_dimension=0, axis_index_groups=column, tiled=True)
    back = lax.all_to_all(total.reshape(EXPERTS, CAP, half), "ctx", 0, 0, axis_index_groups=plane, tiled=True)
    back = back.reshape(EXPERTS * CAP, half)
    own = lax.dot_general(selector, back, (((0,), (0,)), ((), ())), preferred_element_type=jnp.float32)
    mixed = (own * route_gain[:, None]).astype(jnp.bfloat16)
    attended = attention(queries, kv_whole)
    return attended, mixed


def solution(mesh):
    in_specs = (
        P("ctx", "tp"),
        P("ctx", "tp"),
        P("ctx", "tp"),
        P("ctx", "tp"),
        P("ctx", None),
        P("ctx"),
        P("ctx", None, "tp"),
        P("ctx", None, "tp"),
        P("ctx", None, "tp"),
    )
    out_specs = (P("ctx", "tp"), P("ctx", "tp"))
    return jax.shard_map(body, mesh=mesh, in_specs=in_specs, out_specs=out_specs, check_vma=False)
```

time: 415 us -> 336 us (0.81)
  blocking collectives: 230 us -> 18.5 us
  waiting for transfers between devices: 28.3 us -> 209 us
  local copies, waits for them, and re-layouts: 66.2 us -> 11 us
  Pallas kernels: 0 us -> 55 us
  other arithmetic: 25 us -> 3.11 us
  loops' own time: 11.1 us -> 0 us
  matrix products: 26.9 us -> 16.7 us
  starting transfers between devices: 11.6 us -> 7.36 us
    all_to_all x3 -> x1, blocking collectives: 230 us -> 16.2 us  [body(): lax.all_to_all(packed, 'ctx', 0, 0, axis_index_groups=plane, tiled=True)]
    all_gather x2 -> x3, waiting for transfers between devices: 28.3 us -> 154 us  [the longest x1 74.4 us: body(): lax.all_gather(jnp.concatenate([projected_keys, projected_values], axis=1...]
    pallas_call x0 -> x1, Pallas kernels: none -> 55 us  [attention(): pl.pallas_call(functools.partial(attention_kernel, rows, groups, q_heads...]
    reduce_scatter x0 -> x1, waiting for transfers between devices: none -> 54.3 us  [body(): lax.psum_scatter(part, 'ctx', scatter_dimension=0, axis_index_groups=colu...]
    split x2 -> x0, local copies, waits for them, and re-layouts: 13.6 us -> none  [the longest x1 7.89 us: exchange_in_pieces(): jnp.split(parts, piece_ends(parts.shape[cut], pieces), axis=cut)]
    another operation x9 -> x0, loops' own time: 11.1 us -> none  [the longest x1 10.5 us: body(): lax.fori_loop(0, total_rows // block_rows, absorb_block, initial)]
    dynamic_slice x8 -> x0, local copies, waits for them, and re-layouts: 10.2 us -> none  [absorb_block(): lax.dynamic_slice_in_dim(value_whole, block_start, block_rows, 0)]
    dot_general x19 -> x4, matrix products: 24.8 us -> 14.6 us  [the longest x1 6.32 us: body(): gate = jnp.dot(rows, w_gate[0], preferred_element_type=jnp.float32)]
  transfers between devices with their start and end apart: 3 -> 5, of which waited for: 2 -> 4; matrix products, arithmetic and copies ran while one was open for 24% -> 1% of each run, Pallas kernels for 0% -> 16%
where the time goes in v1:
time: 336 us
  waiting for transfers between devices  209 us (62%)
  Pallas kernels  55 us (16%)
  blocking collectives  18.5 us (6%)
  matrix products  16.7 us (5%)
  between operations  15.3 us (5%)
  local copies, waits for them, and re-layouts  11 us (3%)
  starting transfers between devices  7.36 us (2%)
    all_gather x1, waiting for transfers between devices, body(): lax.all_gather(jnp.concatenate([projected_keys, projected_values], axis=1...  74.4 us
    all_gather x1, waiting for transfers between devices, body(): lax.all_gather(arrived, 'ctx', axis=0, axis_index_groups=column, tiled=True)  55.2 us
    pallas_call x1, Pallas kernels, attention(): pl.pallas_call(functools.partial(attention_kernel, rows, groups, q_heads...  55 us
    reduce_scatter x1, waiting for transfers between devices, body(): lax.psum_scatter(part, 'ctx', scatter_dimension=0, axis_index_groups=colu...  54.3 us
    all_gather x1, waiting for transfers between devices, body(): rows = lax.all_gather(rows, 'tp', axis=1, tiled=True)  24.8 us
    all_to_all x1, blocking collectives, body(): lax.all_to_all(packed, 'ctx', 0, 0, axis_index_groups=plane, tiled=True)  16.2 us
    all_to_all x1, starting transfers between devices, body(): lax.all_to_all(total.reshape(EXPERTS, CAP, half), 'ctx', 0, 0, axis_index...  7.2 us
  transfers between devices with their start and end apart: 5, of which 4 were waited for; matrix products, arithmetic and copies ran while one was open for 1% of the time, Pallas kernels for 16%

profile of v1, /device:TPU:30, one launch (start us, length us, event | category | flops | bytes accessed | tf_op | source)
XLA Modules:
  0.0 335.6 jit_solution(14567918620038325264)
XLA Ops:
  8.0 0.0 copy-start
  8.0 0.0 all-gather.6.cloned.1.call-start
  8.1 0.9 fusion.12
  8.9 0.1 reduce_window_sum.11
  9.0 0.8 select_reduce_fusion
  9.9 0.7 multiply_add_fusion
  10.5 2.0 convolution_convert_fusion.1
  12.6 1.2 reshape.25
  13.8 16.2 %all_to_all.10 = bf16[16,6,2560]{2,1,0:T(8,128)(2,1)} all-to-all(bf16[16,6,2560]{2,1,0:T(8,128)(2,1)S(1)} %reshape.25), channel_id=1, replica_groups={{0,16,32,48,64,80,96,112,128,144,160,176,192,208,224,240},{2,18,34,50,6..., dimensions={0} | all-to-all | bytes 983040 | tf_op jit(solution)/shard_map/all_to_all | solution.py:108
  29.9 2.0 reshape.26
  32.0 0.0 all-gather.6.cloned.1.call-update
  32.0 0.0 all-gather.8.cloned.1.call-start
  32.0 55.2 %all-gather.6.cloned.1.call-done = bf16[768,2560]{1,0:T(8,128)(2,1)} async-done(((bf16[96,2560]{1,0:T(8,128)(2,1)}), bf16[768,2560]{1,0:T(8,128)(2,1)}) %all-gather.6.cloned.1.call-update) | async-done | bytes 3932176 | tf_op jit(solution)/shard_map/all_gather | solution.py:110
  87.2 0.0 all-gather.8.cloned.1.call-update
  87.2 0.0 reduce-scatter.2.cloned.1.call-start
  87.3 24.8 %all-gather.8.cloned.1.call-done = bf16[768,5120]{1,0:T(8,128)(2,1)} async-done(((bf16[768,2560]{1,0:T(8,128)(2,1)}), bf16[768,5120]{1,0:T(8,128)(2,1)}) %all-gather.8.cloned.1.call-update) | async-done | bytes 7864336 | tf_op jit(solution)/shard_map/all_gather | solution.py:111
  112.0 0.0 copy-start.6
  112.0 0.0 copy-start.7
  112.0 6.3 %fusion.4 = f32[768,256]{1,0:T(8,128)S(1)} fusion(bf16[768,5120]{1,0:T(8,128)(2,1)} %all-gather.8.cloned.1.call-done, bf16[1,5120,256]{2,1,0:T(8,128)(2,1)} %param.15), kind=kOutput, calls=%fused_computation.7 | convolution fusion | flops 2013265920 | bytes 11272192 | tf_op jit(solution)/shard_map/dot_general | solution.py:112
  118.4 0.0 copy-done.6
  118.4 0.6 copy-done.7
  119.0 2.2 fusion.9
  121.2 2.4 all_gather.15
  123.6 0.0 copy-done
  123.6 4.1 %convolution_convert_fusion = bf16[768,2560]{1,0:T(8,128)(2,1)} fusion(bf16[768,512]{1,0:T(8,128)(2,1)S(1)} %all_gather.15, bf16[1,512,2560]{2,1,0:T(8,128)(2,1)S(1)} %copy-done), kind=kOutput, calls=%fused_computation | convolution fusion | flops 2015232000 | bytes 7340032 | tf_op jit(solution)/shard_map/dot_general | solution.py:116
  127.6 0.0 copy-start.3
  127.6 0.0 copy-start.4
  127.6 0.0 copy-start.2
  127.6 0.0 reduce-scatter.2.cloned.1.call-update
  127.7 0.0 all-gather.4.cloned.1.call-start
  127.7 0.7 copy-done.3
  128.4 0.0 copy-done.4
  128.4 0.6 pad_maximum_fusion
  129.0 0.0 all-gather.4.cloned.1.call-update
  129.1 54.3 %reduce-scatter.2.cloned.1.call-done = bf16[96,2560]{1,0:T(8,128)(2,1)} async-done(((bf16[768,2560]{1,0:T(8,128)(2,1)}), bf16[96,2560]{1,0:T(8,128)(2,1)}) %reduce-scatter.2.cloned.1.call-update) | async-done | bytes 491536 | tf_op jit(solution)/shard_map/reduce_scatter | solution.py:117
  183.4 2.1 reshape.27
  185.5 7.2 %all-to-all-start.1 = ((bf16[16,6,2560]{2,1,0:T(8,128)(2,1)}), bf16[16,6,2560]{2,1,0:T(8,128)(2,1)S(1)}, u32[]{:S(2)}, u32[]{:S(2)}) async-start(bf16[16,6,2560]{2,1,0:T(8,128)(2,1)} %reshape.27), calls=%async_computation.2 | async-start | bytes 1310720 | tf_op jit(solution)/shard_map/all_to_all | solution.py:118
  192.7 74.4 %all-gather.4.cloned.1.call-done.kv_ref = bf16[8192,512]{1,0:T(8,128)(2,1)} async-done(((bf16[64,512]{1,0:T(8,128)(2,1)}), bf16[8192,512]{1,0:T(8,128)(2,1)}) %all-gather.4.cloned.1.call-update) | async-done | bytes 8388624 | tf_op jit(solution)/shard_map/all_gather | solution.py:99
  267.1 0.0 copy-done.2
  267.1 0.0 copy-start.1
  267.1 3.4 %copy-done.1 = bf16[8192,512]{1,0:T(8,128)(2,1)S(1)} copy-done((bf16[8192,512]{1,0:T(8,128)(2,1)S(1)}, bf16[8192,512]{1,0:T(8,128)(2,1)}, u32[]{:S(2)}) %copy-start.1) | copy-done | bytes 8388632
  270.5 0.0 copy-start.5
  270.5 55.0 %attention.1 = bf16[64,1280]{1,0:T(8,128)(2,1)} custom-call(bf16[64,1280]{1,0:T(8,128)(2,1)S(1)} %copy-done.2, bf16[8192,512]{1,0:T(8,128)(2,1)S(1)} %copy-done.1), custom_call_target="tpu_custom_call" | custom-call | flops 2684354560 | bytes 8388608 | tf_op jit(solution)/shard_map/attention/pallas_call | solution.py:74
  325.4 0.0 all-to-all-done.1
  325.4 0.9 reshape.28
  326.4 0.0 copy-done.5
  326.4 2.1 fusion
Async XLA Ops:
  8.0 115.6 %copy-start = (bf16[1,512,2560]{2,1,0:T(8,128)(2,1)S(1)}, bf16[1,512,2560]{2,1,0:T(8,128)(2,1)}, u32[]{:S(2)}) copy-start(bf16[1,512,2560]{2,1,0:T(8,128)(2,1)} %param.17) | copy-start | bytes 7864324
  8.0 79.2 %all-gather.6.cloned.1.call-start = ((), (), s32[]{:S(2)}) async-start(), calls=%async_computation.4 | async-start | bytes 4423680 | tf_op jit(solution)/shard_map/all_gather | solution.py:110
  32.0 80.1 %all-gather.8.cloned.1.call-start = ((), (), s32[]{:S(2)}) async-start(), calls=%async_computation.5 | async-start | bytes 11796480 | tf_op jit(solution)/shard_map/all_gather | solution.py:111
  87.2 96.2 %reduce-scatter.2.cloned.1.call-start = ((), (), s32[]{:S(2)}) async-start(), calls=%async_computation.6 | async-start | bytes 4423680 | tf_op jit(solution)/shard_map/reduce_scatter | solution.py:117
  112.0 6.3 %copy-start.6 = (bf16[768,5120]{1,0:T(8,128)(2,1)S(1)}, bf16[768,5120]{1,0:T(8,128)(2,1)}, u32[]{:S(2)}) copy-start(bf16[768,5120]{1,0:T(8,128)(2,1)} %all-gather.8.cloned.1.call-done) | copy-start | bytes 23592964
  112.0 7.0 %copy-start.7 = (bf16[1,5120,256]{2,1,0:T(8,128)(2,1)S(1)}, bf16[1,5120,256]{2,1,0:T(8,128)(2,1)}, u32[]{:S(2)}) copy-start(bf16[1,5120,256]{2,1,0:T(8,128)(2,1)} %param.16) | copy-start | bytes 7864324
  127.6 0.8 copy-start.3
  127.6 0.8 copy-start.4
  127.6 139.4 %copy-start.2 = (bf16[64,1280]{1,0:T(8,128)(2,1)S(1)}, bf16[64,1280]{1,0:T(8,128)(2,1)}, u32[]{:S(2)}) copy-start(bf16[64,1280]{1,0:T(8,128)(2,1)} %q_ref.1) | copy-start | bytes 491524
  127.7 139.4 %all-gather.4.cloned.1.call-start = ((), (), s32[]{:S(2)}) async-start(), calls=%async_computation.3 | async-start | bytes 8454144 | tf_op jit(solution)/shard_map/all_gather | solution.py:99
  185.5 139.9 %all-to-all-start.1 = ((bf16[16,6,2560]{2,1,0:T(8,128)(2,1)}), bf16[16,6,2560]{2,1,0:T(8,128)(2,1)S(1)}, u32[]{:S(2)}, u32[]{:S(2)}) async-start(bf16[16,6,2560]{2,1,0:T(8,128)(2,1)} %reshape.27), calls=%async_computation.2 | async-start | bytes 1310720 | tf_op jit(solution)/shard_map/all_to_all | solution.py:118
  267.1 3.4 %copy-start.1 = (bf16[8192,512]{1,0:T(8,128)(2,1)S(1)}, bf16[8192,512]{1,0:T(8,128)(2,1)}, u32[]{:S(2)}) copy-start(bf16[8192,512]{1,0:T(8,128)(2,1)} %all-gather.4.cloned.1.call-done.kv_ref) | copy-start | bytes 25165828
  270.5 55.9 %copy-start.5 = (f32[64]{0:T(128)S(1)}, f32[64]{0:T(128)}, u32[]{:S(2)}) copy-start(f32[64]{0:T(128)} %param.14) | copy-start | bytes 772
Sparse Core Ops, SparseCore 0:
  32.1 55.0 all-gather.5
  89.0 23.0 all-gather.7
  127.8 55.5 reduce-scatter.1
Sparse Core Ops, SparseCore 1:
  132.3 134.7 all-gather.3

commit v2 on v1

v2 whole, which is shorter than its diff:
```python
import functools

import jax
import jax.numpy as jnp
from jax import lax
from jax.experimental import pallas as pl
from jax.experimental.pallas import tpu as pltpu
from jax.sharding import PartitionSpec as P

HEAD = 128
EXPERTS = 16
SIDE = 4
HOSTS = 8
CAP = 6
SLOT = 8
LOG2E = 1.4426950408889634
NEG = -1e30
MESH = pl.DeviceIdType.MESH
BF = jnp.bfloat16
F32 = jnp.float32


def iota(shape, dim):
    return lax.broadcasted_iota(jnp.int32, shape, dim)


def dot(a, b):
    return jnp.dot(a, b, preferred_element_type=F32)


def kernel(
    ids_ref, gain_ref, hidden_ref, q_ref, keys_ref, values_ref, wg_ref, wu_ref, wd_ref,
    att_ref, mix_ref,
    packed, a2a_in, rows_all, wgu, wd, inner_all, parts, rs_in, back_out, back_in, sel_ref,
    kv, qs, m_ref, l_ref, acc_ref,
    local_sem, a2a_s, a2a_r, kvz_s, kvz_r, zg_s, zg_r, px_s, px_r, in_s, in_r, kv_s, kv_r, rs_s, rs_r, bk_s, bk_r,
):
    tok, half = hidden_ref.shape
    me = lax.axis_index("ctx")
    core = lax.axis_index("tp")
    z = lax.rem(me, HOSTS)
    p = me // HOSTS
    px, py = p // SIDE, lax.rem(p, SIDE)
    crows = EXPERTS * CAP
    hrows = crows // 2
    block_rows = HOSTS * tok
    kvw = keys_ref.shape[1]
    groups = kvw // HEAD
    heads = q_ref.shape[1] // HEAD // groups

    def zat(d):
        return lax.rem(z + d + HOSTS, HOSTS)

    def dev_z(d):
        return {"ctx": p * HOSTS + zat(d), "tp": core}

    def plane_at(i):
        return lax.rem(p + i, EXPERTS)

    def dev_plane(q):
        return {"ctx": q * HOSTS + z, "tp": core}

    partner = {"ctx": me, "tp": 1 - core}

    def remote(src, dst, s, r, device):
        return pltpu.make_async_remote_copy(
            src_ref=src, dst_ref=dst, send_sem=s, recv_sem=r, device_id=device, device_id_type=MESH
        )

    barrier = pltpu.get_barrier_semaphore()
    greeted = [dev_plane(plane_at(i)) for i in range(1, EXPERTS)] + [dev_z(d) for d in range(1, HOSTS)] + [partner]
    for device in greeted:
        pl.semaphore_signal(barrier, inc=1, device_id=device, device_id_type=MESH)

    own_rows = pl.ds(pl.multiple_of(me * tok, tok), tok)
    local = [
        pltpu.make_async_copy(keys_ref, kv.at[own_rows, pl.ds(0, kvw)], local_sem.at[0]),
        pltpu.make_async_copy(values_ref, kv.at[own_rows, pl.ds(kvw, kvw)], local_sem.at[1]),
        pltpu.make_async_copy(wg_ref.at[0], wgu.at[:, pl.ds(0, wg_ref.shape[2])], local_sem.at[2]),
        pltpu.make_async_copy(wu_ref.at[0], wgu.at[:, pl.ds(wg_ref.shape[2], wg_ref.shape[2])], local_sem.at[3]),
        pltpu.make_async_copy(wd_ref.at[0], wd, local_sem.at[4]),
    ]
    for c in local:
        c.start()

    ids = ids_ref[...]
    chosen = (ids == iota((tok, EXPERTS), 1)).astype(F32)
    before = (iota((tok, tok), 1) < iota((tok, tok), 0)).astype(BF)
    rank = jnp.sum(dot(before, chosen.astype(BF)) * chosen, axis=1, keepdims=True).astype(jnp.int32)
    slot = ids * SLOT + rank
    sel = (slot == iota((tok, EXPERTS * SLOT), 1)).astype(BF)
    sel_ref[...] = sel
    packed[...] = lax.dot_general(
        sel, hidden_ref[...], (((0,), (0,)), ((), ())), preferred_element_type=F32
    ).astype(BF)
    for g in range(groups):
        for h in range(heads):
            i = g * heads + h
            qs[g, h * tok : (h + 1) * tok, :] = q_ref[:, i * HEAD : (i + 1) * HEAD]
    m_ref[...] = jnp.full_like(m_ref, NEG)
    l_ref[...] = jnp.zeros_like(l_ref)
    acc_ref[...] = jnp.zeros_like(acc_ref)

    pl.semaphore_wait(barrier, len(greeted))

    def slot_rows(q):
        return pl.ds(pl.multiple_of(q * SLOT, SLOT), SLOT)

    def a2a(i):
        q = plane_at(i)
        return remote(packed.at[slot_rows(q)], a2a_in.at[slot_rows(p)], a2a_s.at[i], a2a_r.at[i], dev_plane(q))

    for i in range(1, EXPERTS):
        a2a(i).start()
    keep = pltpu.make_async_copy(packed.at[slot_rows(p)], a2a_in.at[slot_rows(p)], local_sem.at[5])
    keep.start()

    local[0].wait()
    local[1].wait()

    def kvz(d):
        return remote(kv.at[own_rows], kv.at[own_rows], kvz_s.at[d], kvz_r.at[d], dev_z(d))

    for d in (1, 7, 2, 6, 3, 5, 4):
        kvz(d).start()

    def shifted(part, d1, d2):
        dx, dy = (d1, d2) if part == 0 else (d2, d1)
        return lax.rem(px + dx + SIDE, SIDE) * SIDE + lax.rem(py + dy + SIDE, SIDE)

    part_rows = block_rows // 2
    unit = part_rows // 2
    kv_copies = {}

    def kv_copy(name, part, along, s, d1, d2, off, n):
        if name not in kv_copies:
            kv_copies[name] = len(kv_copies)
        k = kv_copies[name]
        rows = pl.ds(pl.multiple_of(shifted(part, d1, d2) * block_rows + part * part_rows + off, unit), n)
        to = shifted(part, s, 0) if along == 1 else shifted(part, 0, s)
        return remote(kv.at[rows], kv.at[rows], kv_s.at[k], kv_r.at[k], dev_plane(to))

    stages = {}
    for part in (0, 1):
        for s in (1, -1):
            fo = 0 if s == 1 else unit
            stages.setdefault("s1", []).append((("s1", part, s), part, 1, s, 0, 0, 0, part_rows))
            stages.setdefault("s2own", []).append((("s2own", part, s), part, 2, s, 0, 0, 0, part_rows))
            stages.setdefault("f1", []).append((("f1", part, s), part, 1, s, -s, 0, fo, unit))
            for d1 in (-1, 1):
                stages.setdefault("s2a", []).append((("s2a", part, s, d1), part, 2, s, d1, 0, 0, part_rows))
            stages.setdefault("f2own", []).append((("f2own", part, s), part, 2, s, 0, -s, fo, unit))
            for off in (0, unit):
                stages.setdefault("s2b", []).append((("s2b", part, s, off), part, 2, s, 2, 0, off, unit))
            for d1 in (-1, 1):
                stages.setdefault("f2a", []).append((("f2a", part, s, d1), part, 2, s, d1, -s, fo, unit))
            stages.setdefault("f2b", []).append((("f2b", part, s), part, 2, s, 2, -s, fo, unit))

    def kv_start(*names):
        for name in names:
            for c in stages[name]:
                kv_copy(*c).start()

    def kv_wait(name):
        for key, part, along, s, d1, d2, off, n in stages[name]:
            e1, e2 = (d1 - s, d2) if along == 1 else (d1, d2 - s)
            k = kv_copies[key]
            rows = pl.ds(pl.multiple_of(shifted(part, e1, e2) * block_rows + part * part_rows + off, unit), n)
            to = shifted(part, s, 0) if along == 1 else shifted(part, 0, s)
            remote(kv.at[rows], kv.at[rows], kv_s.at[k], kv_r.at[k], dev_plane(to)).wait_recv()

    def half_of(direction, a):
        return a % 2 if direction == 0 else 1 - a % 2

    def rows_at(zs, h):
        return rows_all.at[core, zs, pl.ds(h * hrows, hrows)]

    def zg_send(direction, n):
        sign = 1 if direction == 0 else -1
        ref = rows_at(zat(-sign * (n // 2)), half_of(direction, n))
        return remote(ref, ref, zg_s.at[direction, n], zg_r.at[direction, n], dev_z(sign))

    def arrived(direction, a):
        sign = 1 if direction == 0 else -1
        return rows_at(zat(-sign * (a // 2 + 1)), half_of(direction, a))

    def zg_wait(direction, a):
        ref = arrived(direction, a)
        sign = 1 if direction == 0 else -1
        remote(ref, ref, zg_s.at[direction, a], zg_r.at[direction, a], dev_z(sign)).wait_recv()

    def px_copy(direction, a):
        ref = arrived(direction, a)
        n = direction * 7 + a
        return remote(ref, ref, px_s.at[n], px_r.at[n], partner)

    def px_wait(direction, a):
        sign = 1 if direction == 0 else -1
        ref = rows_all.at[1 - core, zat(-sign * (a // 2 + 1)), pl.ds(half_of(direction, a) * hrows, hrows)]
        n = direction * 7 + a
        remote(ref, ref, px_s.at[n], px_r.at[n], partner).wait_recv()

    def arrive(a):
        for direction in (0, 1):
            zg_wait(direction, a)
            if a <= 4:
                zg_send(direction, a + 2).start()
            px_copy(direction, a).start()

    def gate_up(zs):
        both = dot(rows_all[0, zs], wgu[:half, :]) + dot(rows_all[1, zs], wgu[half:, :])
        width = both.shape[1] // 2
        gate, up = both[:, :width], both[:, width:]
        inner_all[core, zs] = (gate / (1.0 + jnp.exp(-gate)) * up).astype(BF)

    def inner_copy(zs):
        ref = inner_all.at[core, zs]
        return remote(ref, ref, in_s.at[zs], in_r.at[zs], partner)

    def inner_wait(zs):
        ref = inner_all.at[1 - core, zs]
        remote(ref, ref, in_s.at[zs], in_r.at[zs], partner).wait_recv()

    width = wg_ref.shape[2]

    def down(zs):
        for c in range(0, half, 512):
            cols = slice(c, c + 512)
            parts[zs, :, cols] = (
                dot(inner_all[0, zs], wd[:width, cols]) + dot(inner_all[1, zs], wd[width:, cols])
            ).astype(BF)

    def pair(f, d):
        @pl.loop(0, 2)
        def _(i):
            f(zat((2 * i - 1) * d))

    for i in range(1, EXPERTS):
        remote(packed.at[slot_rows(p)], a2a_in.at[slot_rows(p)], a2a_s.at[i], a2a_r.at[i], dev_plane(plane_at(i))).wait_recv()
    keep.wait()
    col = iota((crows, EXPERTS * SLOT), 1)
    dense = ((col // SLOT) * CAP + lax.rem(col, SLOT) == iota((crows, EXPERTS * SLOT), 0)) & (lax.rem(col, SLOT) < CAP)
    dense = dense.astype(BF)
    for c in range(0, half, 512):
        rows_all[core, z, :, c : c + 512] = dot(dense, a2a_in[:, c : c + 512]).astype(BF)

    for d in range(1, HOSTS):
        rows = pl.ds(pl.multiple_of((p * HOSTS + zat(-d)) * tok, tok), tok)
        remote(kv.at[rows], kv.at[rows], kvz_s.at[d], kvz_r.at[d], dev_z(d)).wait_recv()
    kv_start("s1", "s2own")
    for n in (0, 1):
        for direction in (0, 1):
            zg_send(direction, n).start()
    own_ref = rows_all.at[core, z]
    own_px = remote(own_ref, own_ref, px_s.at[14], px_r.at[14], partner)
    own_px.start()
    other_ref = rows_all.at[1 - core, z]
    local[2].wait()
    local[3].wait()
    local[4].wait()
    remote(other_ref, other_ref, px_s.at[14], px_r.at[14], partner).wait_recv()
    gate_up(z)

    arrive(0)
    kv_wait("s1")
    kv_start("f1", "s2a")
    inner_copy(z).start()

    arrive(1)
    inner_wait(z)
    down(z)
    kv_wait("s2own")
    kv_start("f2own")

    def ready(d):
        for direction in (0, 1):
            px_wait(direction, 2 * d - 2)
            px_wait(direction, 2 * d - 1)

    arrive(2)
    ready(1)
    pair(gate_up, 1)
    kv_wait("f1")
    kv_start("s2b")
    pair(lambda zs: inner_copy(zs).start(), 1)

    arrive(3)
    pair(inner_wait, 1)
    pair(down, 1)
    kv_wait("s2a")
    kv_start("f2a")

    arrive(4)
    ready(2)
    pair(gate_up, 2)
    pair(lambda zs: inner_copy(zs).start(), 2)

    arrive(5)
    pair(inner_wait, 2)
    pair(down, 2)
    ready(3)
    pair(gate_up, 3)
    kv_wait("s2b")
    kv_start("f2b")
    pair(lambda zs: inner_copy(zs).start(), 3)

    arrive(6)
    pair(inner_wait, 3)
    pair(down, 3)

    def rs_ref(direction, n):
        sign = 1 if direction == 0 else -1
        return parts.at[zat(sign * (4 - (n + 1) // 2)), pl.ds(half_of(direction, n) * hrows, hrows)]

    def rs_send(direction, n):
        sign = 1 if direction == 0 else -1
        return remote(rs_ref(direction, n), rs_in.at[direction, n], rs_s.at[direction, n], rs_r.at[direction, n], dev_z(sign))

    def rs_step(n):
        for direction in (0, 1):
            rs_send(direction, n - 2).wait_recv()
            ref = rs_ref(direction, n)
            ref[...] = (ref[...].astype(F32) + rs_in[direction, n - 2].astype(F32)).astype(BF)

    def rs_go(n):
        for direction in (0, 1):
            rs_send(direction, n).start()

    px_wait(0, 6)
    px_wait(1, 6)
    rs_go(1)
    far = zat(4)
    gate_up(far)
    kv_wait("f2own")
    inner_copy(far).start()
    inner_wait(far)
    down(far)

    scale = HEAD ** (-0.5) * LOG2E

    def attend(b, masked):
        rows = pl.ds(pl.multiple_of(b * block_rows, block_rows), block_rows)
        for g in range(groups):
            k = kv[rows, g * HEAD : (g + 1) * HEAD]
            v = kv[rows, kvw + g * HEAD : kvw + (g + 1) * HEAD]
            s = lax.dot_general(qs[g], k, (((1,), (1,)), ((), ())), preferred_element_type=F32) * scale
            if masked:
                row = z * tok + lax.rem(iota(s.shape, 0), tok)
                s = jnp.where(iota(s.shape, 1) <= row, s, NEG)
            tiles = [s[:, j : j + HEAD] for j in range(0, block_rows, HEAD)]
            top = functools.reduce(jnp.maximum, tiles)
            m_old = m_ref[g]
            m_new = jnp.maximum(m_old, jnp.max(top, axis=1, keepdims=True))
            w = [jnp.exp2(t - m_new) for t in tiles]
            f = jnp.exp2(m_old - m_new)
            m_ref[g] = m_new
            l_ref[g] = l_ref[g] * f + functools.reduce(jnp.add, w)
            wb = jnp.concatenate([t.astype(BF) for t in w], axis=1)
            acc_ref[g] = acc_ref[g] * f + dot(wb, v)

    def attend_share(n, of):
        @pl.loop(p * n // of, p * (n + 1) // of)
        def _(b):
            attend(b, False)

    kv_wait("f2a")
    rs_go(0)
    rs_step(3)
    attend(p, True)
    rs_go(3)
    rs_step(2)
    kv_wait("f2b")
    rs_go(2)
    attend_share(0, 4)
    rs_step(5)
    rs_go(5)
    attend_share(1, 4)
    rs_step(4)
    rs_go(4)
    attend_share(2, 4)
    rs_step(6)
    rs_go(6)
    attend_share(3, 4)
    for g in range(groups):
        out = acc_ref[g] / jnp.sum(l_ref[g], axis=1, keepdims=True)
        for h in range(heads):
            i = g * heads + h
            att_ref[:, i * HEAD : (i + 1) * HEAD] = out[h * tok : (h + 1) * tok].astype(BF)

    for n in (5, 6):
        for direction in (0, 1):
            rs_send(direction, n).wait_recv()
    srow = iota((EXPERTS * SLOT // 2, hrows), 0)
    spread = ((srow // SLOT) * CAP + lax.rem(srow, SLOT) == iota((EXPERTS * SLOT // 2, hrows), 1)) & (
        lax.rem(srow, SLOT) < CAP
    )
    spread = spread.astype(BF)
    for h in (0, 1):
        right, left = (6, 5) if h == 0 else (5, 6)
        total = (
            parts[z, h * hrows : (h + 1) * hrows, :].astype(F32)
            + rs_in[0, right].astype(F32)
            + rs_in[1, left].astype(F32)
        ).astype(BF)
        n = EXPERTS * SLOT // 2
        back_out[h * n : (h + 1) * n, :] = dot(spread, total).astype(BF)

    def back(i):
        q = plane_at(i)
        return remote(back_out.at[slot_rows(q)], back_in.at[slot_rows(p)], bk_s.at[i], bk_r.at[i], dev_plane(q))

    for i in range(1, EXPERTS):
        back(i).start()
    stay = pltpu.make_async_copy(back_out.at[slot_rows(p)], back_in.at[slot_rows(p)], local_sem.at[6])
    stay.start()

    for i in range(1, EXPERTS):
        a2a(i).wait_send()
    for d in range(1, HOSTS):
        kvz(d).wait_send()
    for n in range(7):
        for direction in (0, 1):
            zg_send(direction, n).wait_send()
            px_copy(direction, n).wait_send()
            rs_send(direction, n).wait_send()
    own_px.wait_send()
    for zs in range(HOSTS):
        inner_copy(zs).wait_send()
    for name in stages:
        for c in stages[name]:
            kv_copy(*c).wait_send()

    for i in range(1, EXPERTS):
        back(i).wait_recv()
    stay.wait()
    for c in range(0, half, 512):
        own = dot(sel_ref[...], back_in[:, c : c + 512])
        mix_ref[:, c : c + 512] = (own * gain_ref[...]).astype(BF)
    for i in range(1, EXPERTS):
        back(i).wait_send()


def body(queries, keys, values, hidden, route_ids, route_gain, w_gate, w_up, w_down):
    tok, half = hidden.shape
    width_q, kvw = queries.shape[1], keys.shape[1]
    ff = w_gate.shape[2]
    total = tok * HOSTS * EXPERTS
    crows = EXPERTS * CAP
    groups = kvw // HEAD
    qrows = width_q // kvw * tok
    vm = pl.BlockSpec(memory_space=pltpu.VMEM)
    hbm = pl.BlockSpec(memory_space=pl.ANY)
    dma = pltpu.SemaphoreType.DMA
    return pl.pallas_call(
        kernel,
        name="layer",
        out_shape=(
            jax.ShapeDtypeStruct((tok, width_q), BF),
            jax.ShapeDtypeStruct((tok, half), BF),
        ),
        in_specs=[vm, vm, vm, vm, hbm, hbm, hbm, hbm, hbm],
        out_specs=(vm, vm),
        scratch_shapes=[
            pltpu.VMEM((EXPERTS * SLOT, half), BF),
            pltpu.VMEM((EXPERTS * SLOT, half), BF),
            pltpu.VMEM((2, HOSTS, crows, half), BF),
            pltpu.VMEM((2 * half, 2 * ff), BF),
            pltpu.VMEM((2 * ff, half), BF),
            pltpu.VMEM((2, HOSTS, crows, ff), BF),
            pltpu.VMEM((HOSTS, crows, half), BF),
            pltpu.VMEM((2, 7, crows // 2, half), BF),
            pltpu.VMEM((EXPERTS * SLOT, half), BF),
            pltpu.VMEM((EXPERTS * SLOT, half), BF),
            pltpu.VMEM((tok, EXPERTS * SLOT), BF),
            pltpu.VMEM((total, 2 * kvw), BF),
            pltpu.VMEM((groups, qrows, HEAD), BF),
            pltpu.VMEM((groups, qrows, HEAD), F32),
            pltpu.VMEM((groups, qrows, HEAD), F32),
            pltpu.VMEM((groups, qrows, HEAD), F32),
            dma((7,)),
            dma((EXPERTS,)), dma((EXPERTS,)),
            dma((HOSTS,)), dma((HOSTS,)),
            dma((2, 7)), dma((2, 7)),
            dma((15,)), dma((15,)),
            dma((HOSTS,)), dma((HOSTS,)),
            dma((44,)), dma((44,)),
            dma((2, 7)), dma((2, 7)),
            dma((EXPERTS,)), dma((EXPERTS,)),
        ],
        compiler_params=pltpu.CompilerParams(
            collective_id=0, has_side_effects=True, vmem_limit_bytes=60 * 1024 * 1024
        ),
    )(route_ids, route_gain[:, None], hidden, queries, keys, values, w_gate, w_up, w_down)


def solution(mesh):
    in_specs = (
        P("ctx", "tp"),
        P("ctx", "tp"),
        P("ctx", "tp"),
        P("ctx", "tp"),
        P("ctx", None),
        P("ctx"),
        P("ctx", None, "tp"),
        P("ctx", None, "tp"),
        P("ctx", None, "tp"),
    )
    out_specs = (P("ctx", "tp"), P("ctx", "tp"))
    return jax.shard_map(body, mesh=mesh, in_specs=in_specs, out_specs=out_specs, check_vma=False)
```

time: 336 us -> 125 us (0.37)
  waiting for transfers between devices: 209 us -> 0 us
  Pallas kernels: 55 us -> 117 us
  blocking collectives: 18.5 us -> 0 us
  matrix products: 16.7 us -> 0 us
  between operations: 15.3 us -> 0.64 us
  starting transfers between devices: 7.36 us -> 0 us
  local copies, waits for them, and re-layouts: 11 us -> 6.03 us
    all_gather x3 -> x0, waiting for transfers between devices: 154 us -> none  [the longest x1 74.4 us: body(): lax.all_gather(jnp.concatenate([projected_keys, projected_values], axis=1...]
    pallas_call x1, Pallas kernels: 55 us -> 117 us  [body(): pl.pallas_call(kernel, name='layer', out_shape=(jax.ShapeDtypeStruct((tok...]
    reduce_scatter x1 -> x0, waiting for transfers between devices: 54.3 us -> none  [body(): lax.psum_scatter(part, 'ctx', scatter_dimension=0, axis_index_groups=colu...]
    dot_general x5 -> x0, matrix products: 16.7 us -> none  [the longest x1 6.32 us: body(): gate = jnp.dot(rows, w_gate[0], preferred_element_type=jnp.float32)]
    all_to_all x1 -> x0, blocking collectives: 16.2 us -> none  [body(): lax.all_to_all(packed, 'ctx', 0, 0, axis_index_groups=plane, tiled=True)]
    all_to_all x1 -> x0, starting transfers between devices: 7.2 us -> none  [body(): lax.all_to_all(total.reshape(EXPERTS, CAP, half), 'ctx', 0, 0, axis_index...]
    reshape x4 -> x0, local copies, waits for them, and re-layouts: 6.25 us -> none  [the longest x1 2.08 us: body(): total.reshape(EXPERTS, CAP, half)]
  transfers between devices with their start and end apart: 5 -> 0, of which waited for: 4 -> 0; matrix products, arithmetic and copies ran while one was open for 1% -> 0% of each run, Pallas kernels for 16% -> 0%
where the time goes in v2:
time: 125 us; the launch traced here: 123 us
  Pallas kernels  117 us (94%)
  local copies, waits for them, and re-layouts  6.03 us (5%)
    pallas_call x1, Pallas kernels, body(): pl.pallas_call(kernel, name='layer', out_shape=(jax.ShapeDtypeStruct((tok...  117 us
    unnamed x3, local copies, waits for them, and re-layouts  4.67 us

profile of v2, /device:TPU:30, one launch (start us, length us, event | category | flops | bytes accessed | tf_op | source)
XLA Modules:
  0.0 123.3 jit_solution(13397862555547178704)
XLA Ops:
  0.6 1.4 %copy.11.ids_ref = s32[64,1]{1,0:T(8,128)} copy(s32[64,1]{0,1:T(1,128)} %param.13) | data formatting | bytes 512 | tf_op args[4]
  2.0 1.4 %copy.12.gain_ref = f32[64,1]{1,0:T(8,128)} copy(f32[64,1]{0,1:T(1,128)} %bitcast.1) | data formatting | bytes 512 | tf_op jit(solution)/shard_map/broadcast_in_dim | solution.py:493
  3.3 116.6 %layer.1 = (bf16[64,1280]{1,0:T(8,128)(2,1)}, bf16[64,2560]{1,0:T(8,128)(2,1)}) custom-call(s32[64,1]{1,0:T(8,128)} %copy.11.ids_ref, f32[64,1]{1,0:T(8,128)} %copy.12.gain_ref, bf16[64,2560]{1,0:T(8,128)(2,1)} %hidden_ref.1, bf16[64,1280]{1,0:T(8,128)(2,1)} %q_ref.1, bf16[64,256]{1,0:T(8,128)(2,1)} %keys_ref.1, bf16[64,256]{1,0:T(8,128)(2,1)} %values_ref.1, ...), custom_call_target="tpu_custom_call" | custom-call | tf_op jit(solution)/shard_map/layer/pallas_call | solution.py:454
  120.0 1.6 %copy.15 = bf16[64,1280]{1,0:T(8,128)(2,1)} copy(bf16[64,1280]{1,0:T(8,128)(2,1)} %get-tuple-element.4) | data formatting | bytes 327680
  121.6 1.7 %copy.16 = bf16[64,2560]{1,0:T(8,128)(2,1)} copy(bf16[64,2560]{1,0:T(8,128)(2,1)} %get-tuple-element.5) | data formatting | bytes 655360

commit v3 on v2

v3 whole, which is shorter than its diff:
```python
import functools

import jax
import jax.numpy as jnp
from jax import lax
from jax.experimental import pallas as pl
from jax.experimental.pallas import tpu as pltpu
from jax.sharding import PartitionSpec as P

HEAD = 128
EXPERTS = 16
SIDE = 4
HOSTS = 8
CAP = 6
SLOT = 8
LOG2E = 1.4426950408889634
NEG = -1e30
MESH = pl.DeviceIdType.MESH
BF = jnp.bfloat16
F32 = jnp.float32


def iota(shape, dim):
    return lax.broadcasted_iota(jnp.int32, shape, dim)


def dot(a, b):
    return jnp.dot(a, b, preferred_element_type=F32)


def kernel(
    ids_ref, gain_ref, hidden_ref, q_ref, keys_ref, values_ref, wg_ref, wu_ref, wd_ref,
    att_ref, mix_ref,
    hid, qin, packed, a2a_in, rows_all, wgu, wd, inner_all, parts, rs_in, back_out, back_in, sel_ref, gain_col,
    kv, qs, m_ref, l_ref, acc_ref,
    local_sem, a2a_s, a2a_r, kvz_s, kvz_r, zg_s, zg_r, px_s, px_r, in_s, in_r, kv_s, kv_r, rs_s, rs_r, bk_s, bk_r,
):
    tok, half = hidden_ref.shape
    me = lax.axis_index("ctx")
    core = lax.axis_index("tp")
    z = lax.rem(me, HOSTS)
    p = me // HOSTS
    px, py = p // SIDE, lax.rem(p, SIDE)
    crows = EXPERTS * CAP
    hrows = crows // 2
    block_rows = HOSTS * tok
    kvw = keys_ref.shape[1]
    groups = kvw // HEAD
    heads = q_ref.shape[1] // HEAD // groups
    width = wg_ref.shape[2]
    chalf, quarter = half // 2, half // 4

    def zat(d):
        return lax.rem(z + d + HOSTS, HOSTS)

    def dev_z(d):
        return {"ctx": p * HOSTS + zat(d), "tp": core}

    def plane_at(i):
        return lax.rem(p + i, EXPERTS)

    def dev_plane(q):
        return {"ctx": q * HOSTS + z, "tp": core}

    partner = {"ctx": me, "tp": 1 - core}
    signs = (1, -1)

    def remote(src, dst, s, r, device):
        return pltpu.make_async_remote_copy(
            src_ref=src, dst_ref=dst, send_sem=s, recv_sem=r, device_id=device, device_id_type=MESH
        )

    barrier = pltpu.get_barrier_semaphore()
    greeted = [dev_plane(plane_at(i)) for i in range(1, EXPERTS)] + [dev_z(1), dev_z(-1), partner]
    for device in greeted:
        pl.semaphore_signal(barrier, inc=1, device_id=device, device_id_type=MESH)

    own_rows = pl.ds(pl.multiple_of(me * tok, tok), tok)
    local = [
        pltpu.make_async_copy(hidden_ref, hid, local_sem.at[0]),
        pltpu.make_async_copy(keys_ref, kv.at[own_rows, pl.ds(0, kvw)], local_sem.at[1]),
        pltpu.make_async_copy(values_ref, kv.at[own_rows, pl.ds(kvw, kvw)], local_sem.at[2]),
        pltpu.make_async_copy(q_ref, qin, local_sem.at[3]),
        pltpu.make_async_copy(wg_ref.at[0], wgu.at[:, pl.ds(0, width)], local_sem.at[4]),
        pltpu.make_async_copy(wu_ref.at[0], wgu.at[:, pl.ds(width, width)], local_sem.at[5]),
        pltpu.make_async_copy(wd_ref.at[0], wd, local_sem.at[6]),
    ]
    for c in local:
        c.start()

    ids = ids_ref[...]
    chosen = (ids == iota((EXPERTS, tok), 0)).astype(F32)
    before = (iota((tok, tok), 0) < iota((tok, tok), 1)).astype(BF)
    rank = jnp.sum(dot(chosen.astype(BF), before) * chosen, axis=0, keepdims=True).astype(jnp.int32)
    sel = (ids * SLOT + rank == iota((EXPERTS * SLOT, tok), 0)).astype(F32)
    sel_ref[...] = sel.T.astype(BF)
    gain_col[...] = jnp.broadcast_to(gain_ref[...], (HEAD, tok)).T
    sel = sel.astype(BF)
    local[0].wait()
    for c in range(0, half, quarter):
        packed[:, c : c + quarter] = dot(sel, hid[:, c : c + quarter]).astype(BF)
    m_ref[...] = jnp.full_like(m_ref, NEG)
    l_ref[...] = jnp.zeros_like(l_ref)
    acc_ref[...] = jnp.zeros_like(acc_ref)
    local[1].wait()
    local[2].wait()

    pl.semaphore_wait(barrier, len(greeted))

    def kvz(direction, n, lag):
        sign = signs[direction]
        start = (p * HOSTS + zat(-sign * (n + lag))) * tok
        if n == 3:
            rows = pl.ds(pl.multiple_of(start + direction * (tok // 2), tok // 2), tok // 2)
        else:
            rows = pl.ds(pl.multiple_of(start, tok), tok)
        return remote(kv.at[rows], kv.at[rows], kvz_s.at[direction, n], kvz_r.at[direction, n], dev_z(sign))

    def kvz_go(n):
        for direction in (0, 1):
            kvz(direction, n, 0).start()

    def kvz_wait(n):
        for direction in (0, 1):
            kvz(direction, n, 1).wait_recv()

    kvz_go(0)

    def slot_rows(q):
        return pl.ds(pl.multiple_of(q * SLOT, SLOT), SLOT)

    def a2a(i, c):
        q = plane_at(i)
        cols = pl.ds(c * quarter, quarter)
        return remote(
            packed.at[slot_rows(q), cols], a2a_in.at[slot_rows(p), cols], a2a_s.at[c, i], a2a_r.at[c, i], dev_plane(q)
        )

    keep = pltpu.make_async_copy(packed.at[slot_rows(p)], a2a_in.at[slot_rows(p)], local_sem.at[7])
    keep.start()
    for c in range(4):
        for i in range(1, EXPERTS):
            a2a(i, c).start()

    def shifted(part, d1, d2):
        dx, dy = (d1, d2) if part == 0 else (d2, d1)
        return lax.rem(px + dx + SIDE, SIDE) * SIDE + lax.rem(py + dy + SIDE, SIDE)

    part_rows = block_rows // 2
    unit = part_rows // 2
    kv_copies = {}

    def kv_copy(name, part, along, s, d1, d2, off, n):
        if name not in kv_copies:
            kv_copies[name] = len(kv_copies)
        k = kv_copies[name]
        rows = pl.ds(pl.multiple_of(shifted(part, d1, d2) * block_rows + part * part_rows + off, unit), n)
        to = shifted(part, s, 0) if along == 1 else shifted(part, 0, s)
        return remote(kv.at[rows], kv.at[rows], kv_s.at[k], kv_r.at[k], dev_plane(to))

    stages = {}
    for part in (0, 1):
        for s in (1, -1):
            fo = 0 if s == 1 else unit
            stages.setdefault("s1", []).append((("s1", part, s), part, 1, s, 0, 0, 0, part_rows))
            stages.setdefault("s2own", []).append((("s2own", part, s), part, 2, s, 0, 0, 0, part_rows))
            stages.setdefault("f1", []).append((("f1", part, s), part, 1, s, -s, 0, fo, unit))
            for d1 in (-1, 1):
                stages.setdefault("s2a", []).append((("s2a", part, s, d1), part, 2, s, d1, 0, 0, part_rows))
            stages.setdefault("f2own", []).append((("f2own", part, s), part, 2, s, 0, -s, fo, unit))
            for off in (0, unit):
                stages.setdefault("s2b", []).append((("s2b", part, s, off), part, 2, s, 2, 0, off, unit))
            for d1 in (-1, 1):
                stages.setdefault("f2a", []).append((("f2a", part, s, d1), part, 2, s, d1, -s, fo, unit))
            stages.setdefault("f2b", []).append((("f2b", part, s), part, 2, s, 2, -s, fo, unit))

    def kv_start(*names):
        for name in names:
            for c in stages[name]:
                kv_copy(*c).start()

    def kv_wait(name):
        for key, part, along, s, d1, d2, off, n in stages[name]:
            e1, e2 = (d1 - s, d2) if along == 1 else (d1, d2 - s)
            k = kv_copies[key]
            rows = pl.ds(pl.multiple_of(shifted(part, e1, e2) * block_rows + part * part_rows + off, unit), n)
            to = shifted(part, s, 0) if along == 1 else shifted(part, 0, s)
            remote(kv.at[rows], kv.at[rows], kv_s.at[k], kv_r.at[k], dev_plane(to)).wait_recv()

    def zg_ref(direction, n, lag):
        sign = signs[direction]
        if n < 4:
            hop, cols, rows = 0, pl.ds(n * quarter, quarter), pl.ds(0, crows)
        else:
            hop, cols = (n - 2) // 2, pl.ds(n % 2 * chalf, chalf)
            rows = pl.ds(direction * hrows, hrows) if n >= 8 else pl.ds(0, crows)
        return rows_all.at[core, zat(-sign * (hop + lag)), rows, cols]

    def zg(direction, n, lag):
        ref = zg_ref(direction, n, lag)
        return remote(ref, ref, zg_s.at[direction, n], zg_r.at[direction, n], dev_z(signs[direction]))

    def px_ref(direction, a, side):
        d, c = a // 2 + 1, a % 2
        rows = pl.ds(direction * hrows, hrows) if d == 4 else pl.ds(0, crows)
        return rows_all.at[side, zat(-signs[direction] * d), rows, pl.ds(c * chalf, chalf)]

    def px_copy(direction, a):
        ref = px_ref(direction, a, core)
        return remote(ref, ref, px_s.at[direction * 8 + a], px_r.at[direction * 8 + a], partner)

    def px_wait(direction, a):
        ref = px_ref(direction, a, 1 - core)
        remote(ref, ref, px_s.at[direction * 8 + a], px_r.at[direction * 8 + a], partner).wait_recv()

    def arrive(a):
        for direction in (0, 1):
            for n in (2 * a, 2 * a + 1) if a < 2 else (a + 2,):
                zg(direction, n, 1).wait_recv()
            if a < 6:
                zg(direction, a + 4, 0).start()
            px_copy(direction, a).start()

    def ready(d):
        for direction in (0, 1):
            px_wait(direction, 2 * d - 2)
            px_wait(direction, 2 * d - 1)

    def gate_up(zs):
        both = dot(rows_all[0, zs], wgu[:half, :]) + dot(rows_all[1, zs], wgu[half:, :])
        gate, up = both[:, :width], both[:, width:]
        inner_all[core, zs] = (gate / (1.0 + jnp.exp(-gate)) * up).astype(BF)

    def inner_copy(zs):
        ref = inner_all.at[core, zs]
        return remote(ref, ref, in_s.at[zs], in_r.at[zs], partner)

    def inner_wait(zs):
        ref = inner_all.at[1 - core, zs]
        remote(ref, ref, in_s.at[zs], in_r.at[zs], partner).wait_recv()

    def down(zs):
        for c in range(0, half, 512):
            cols = slice(c, c + 512)
            parts[zs, :, cols] = (
                dot(inner_all[0, zs], wd[:width, cols]) + dot(inner_all[1, zs], wd[width:, cols])
            ).astype(BF)

    def pair(f, d):
        @pl.loop(0, 2)
        def _(i):
            f(zat((2 * i - 1) * d))

    col = iota((crows, EXPERTS * SLOT), 1)
    dense = ((col // SLOT) * CAP + lax.rem(col, SLOT) == iota((crows, EXPERTS * SLOT), 0)) & (lax.rem(col, SLOT) < CAP)
    dense = dense.astype(BF)
    kvz_wait(0)
    kvz_go(1)
    keep.wait()
    for c in range(4):
        cols = pl.ds(c * quarter, quarter)
        for i in range(1, EXPERTS):
            ref = a2a_in.at[slot_rows(plane_at(EXPERTS - i)), cols]
            remote(ref, ref, a2a_s.at[c, i], a2a_r.at[c, i], dev_plane(plane_at(i))).wait_recv()
        rows_all[core, z, :, c * quarter : (c + 1) * quarter] = dot(
            dense, a2a_in[:, c * quarter : (c + 1) * quarter]
        ).astype(BF)
        if c in (0, 1):
            kvz_wait(c + 1)
            kvz_go(c + 2)
        for direction in (0, 1):
            zg(direction, c, 0).start()
    own_ref = rows_all.at[core, z]
    own_px = remote(own_ref, own_ref, px_s.at[16], px_r.at[16], partner)
    own_px.start()
    kvz_wait(3)
    kv_start("s1", "s2own")
    local[3].wait()
    for g in range(groups):
        for h in range(heads):
            i = g * heads + h
            qs[g, h * tok : (h + 1) * tok, :] = qin[:, i * HEAD : (i + 1) * HEAD]
    other_ref = rows_all.at[1 - core, z]
    local[4].wait()
    local[5].wait()
    local[6].wait()

    arrive(0)
    remote(other_ref, other_ref, px_s.at[16], px_r.at[16], partner).wait_recv()
    gate_up(z)
    kv_wait("s1")
    kv_start("f1", "s2a")
    inner_copy(z).start()

    arrive(1)
    inner_wait(z)
    down(z)
    kv_wait("s2own")
    kv_start("f2own")

    arrive(2)
    ready(1)
    pair(gate_up, 1)
    kv_wait("f1")
    kv_start("s2b")
    pair(lambda zs: inner_copy(zs).start(), 1)

    arrive(3)
    pair(inner_wait, 1)
    pair(down, 1)
    kv_wait("s2a")
    kv_start("f2a")

    arrive(4)
    ready(2)
    pair(gate_up, 2)
    pair(lambda zs: inner_copy(zs).start(), 2)

    arrive(5)
    pair(inner_wait, 2)
    pair(down, 2)
    ready(3)
    pair(gate_up, 3)
    pair(lambda zs: inner_copy(zs).start(), 3)

    def rs_rows(direction, chain):
        return pl.ds((direction ^ chain) * hrows, hrows)

    def rs_part(direction, chain, t, c):
        return parts.at[zat(signs[direction] * t), rs_rows(direction, chain), pl.ds(c * chalf, chalf)]

    def rs_slot(direction, chain, t, c):
        return rs_in.at[direction, chain * 4 + t - 1, :, pl.ds(c * chalf, chalf)]

    def rs(direction, chain, t, c):
        n = (chain * 4 + t - 1) * 2 + c
        return remote(
            rs_part(direction, chain, t, c), rs_slot(direction, chain, t, c),
            rs_s.at[direction, n], rs_r.at[direction, n], dev_z(signs[direction]),
        )

    def rs_add(chain, t, c):
        for direction in (0, 1):
            rs(direction, chain, t + 1, c).wait_recv()
            ref = rs_part(direction, chain, t, c)
            ref[...] = (ref[...].astype(F32) + rs_slot(direction, chain, t + 1, c)[...].astype(F32)).astype(BF)

    def rs_go(chain, t, c):
        for direction in (0, 1):
            rs(direction, chain, t, c).start()

    def rs_step(chain, t, c):
        rs_add(chain, t, c)
        rs_go(chain, t, c)

    scale = HEAD ** (-0.5) * LOG2E

    def attend(b, masked):
        rows = pl.ds(pl.multiple_of(b * block_rows, block_rows), block_rows)
        for g in range(groups):
            k = kv[rows, g * HEAD : (g + 1) * HEAD]
            v = kv[rows, kvw + g * HEAD : kvw + (g + 1) * HEAD]
            s = lax.dot_general(qs[g], k, (((1,), (1,)), ((), ())), preferred_element_type=F32) * scale
            if masked:
                row = z * tok + lax.rem(iota(s.shape, 0), tok)
                s = jnp.where(iota(s.shape, 1) <= row, s, NEG)
            tiles = [s[:, j : j + HEAD] for j in range(0, block_rows, HEAD)]
            top = functools.reduce(jnp.maximum, tiles)
            m_old = m_ref[g]
            m_new = jnp.maximum(m_old, jnp.max(top, axis=1, keepdims=True))
            w = [jnp.exp2(t - m_new) for t in tiles]
            f = jnp.exp2(m_old - m_new)
            m_ref[g] = m_new
            l_ref[g] = l_ref[g] * f + functools.reduce(jnp.add, w)
            wb = jnp.concatenate([t.astype(BF) for t in w], axis=1)
            acc_ref[g] = acc_ref[g] * f + dot(wb, v)

    def attend_share(n, of):
        @pl.loop(p * n // of, p * (n + 1) // of)
        def _(b):
            attend(b, False)

    arrive(6)
    pair(inner_wait, 3)
    pair(down, 3)
    rs_go(1, 3, 0)
    rs_go(1, 3, 1)
    arrive(7)
    far = zat(4)
    ready(4)
    gate_up(far)
    inner_copy(far).start()
    kv_wait("s2b")
    kv_start("f2b")
    inner_wait(far)
    down(far)
    kv_wait("f2own")
    rs_go(0, 4, 0)
    rs_step(1, 2, 0)
    rs_go(0, 4, 1)
    rs_step(1, 2, 1)
    attend(p, True)
    kv_wait("f2a")
    rs_step(0, 3, 0)
    kv_wait("f2b")
    attend_share(0, 4)
    rs_step(0, 3, 1)
    rs_step(1, 1, 0)
    attend_share(1, 4)
    rs_step(0, 2, 0)
    rs_step(0, 2, 1)
    attend_share(2, 4)
    rs_step(0, 1, 0)
    rs_step(1, 1, 1)
    rs_step(0, 1, 1)
    attend_share(3, 4)

    srow = iota((EXPERTS * SLOT // 2, hrows), 0)
    spread = ((srow // SLOT) * CAP + lax.rem(srow, SLOT) == iota((EXPERTS * SLOT // 2, hrows), 1)) & (
        lax.rem(srow, SLOT) < CAP
    )
    spread = spread.astype(BF)

    def back(i, c):
        q = plane_at(i)
        cols = pl.ds(c * chalf, chalf)
        return remote(
            back_out.at[slot_rows(q), cols], back_in.at[slot_rows(p), cols], bk_s.at[c, i], bk_r.at[c, i], dev_plane(q)
        )

    def finish(c):
        for direction in (0, 1):
            rs(direction, 1, 1, c).wait_recv()
            rs(direction, 0, 1, c).wait_recv()
        cols = slice(c * chalf, (c + 1) * chalf)
        for h in (0, 1):
            total = parts[z, h * hrows : (h + 1) * hrows, cols].astype(F32)
            for direction in (0, 1):
                total = total + rs_slot(direction, direction ^ h, 1, c)[...].astype(F32)
            n = EXPERTS * SLOT // 2
            back_out[h * n : (h + 1) * n, cols] = dot(spread, total.astype(BF)).astype(BF)
        stay = pltpu.make_async_copy(
            back_out.at[slot_rows(p), pl.ds(c * chalf, chalf)],
            back_in.at[slot_rows(p), pl.ds(c * chalf, chalf)],
            local_sem.at[8 + c],
        )
        stay.start()
        for i in range(1, EXPERTS):
            back(i, c).start()
        return stay

    def mix(c, stay):
        for i in range(1, EXPERTS):
            ref = back_in.at[slot_rows(plane_at(EXPERTS - i)), pl.ds(c * chalf, chalf)]
            remote(ref, ref, bk_s.at[c, i], bk_r.at[c, i], dev_plane(plane_at(i))).wait_recv()
        stay.wait()
        for b in range(c * chalf, (c + 1) * chalf, quarter):
            own = dot(sel_ref[...], back_in[:, b : b + quarter])
            for t in range(0, quarter, HEAD):
                mix_ref[:, b + t : b + t + HEAD] = (own[:, t : t + HEAD] * gain_col[...]).astype(BF)

    first = finish(0)
    for g in range(groups):
        out = acc_ref[g] / jnp.sum(l_ref[g], axis=1, keepdims=True)
        for h in range(heads):
            i = g * heads + h
            att_ref[:, i * HEAD : (i + 1) * HEAD] = out[h * tok : (h + 1) * tok].astype(BF)
    second = finish(1)

    for c in range(4):
        for i in range(1, EXPERTS):
            a2a(i, c).wait_send()
    for direction in (0, 1):
        for n in range(4):
            kvz(direction, n, 0).wait_send()
        for n in range(10):
            zg(direction, n, 0).wait_send()
        for a in range(8):
            px_copy(direction, a).wait_send()
        for c in (0, 1):
            for t in (4, 3, 2, 1):
                rs(direction, 0, t, c).wait_send()
            for t in (3, 2, 1):
                rs(direction, 1, t, c).wait_send()
    own_px.wait_send()
    for zs in range(HOSTS):
        inner_copy(zs).wait_send()
    for name in stages:
        for c in stages[name]:
            kv_copy(*c).wait_send()

    mix(0, first)
    mix(1, second)
    for c in (0, 1):
        for i in range(1, EXPERTS):
            back(i, c).wait_send()


def body(queries, keys, values, hidden, route_ids, route_gain, w_gate, w_up, w_down):
    tok, half = hidden.shape
    width_q, kvw = queries.shape[1], keys.shape[1]
    ff = w_gate.shape[2]
    total = tok * HOSTS * EXPERTS
    crows = EXPERTS * CAP
    groups = kvw // HEAD
    qrows = width_q // kvw * tok
    vm = pl.BlockSpec(memory_space=pltpu.VMEM)
    hbm = pl.BlockSpec(memory_space=pl.ANY)
    dma = pltpu.SemaphoreType.DMA
    return pl.pallas_call(
        kernel,
        name="layer",
        out_shape=(
            jax.ShapeDtypeStruct((tok, width_q), BF),
            jax.ShapeDtypeStruct((tok, half), BF),
        ),
        in_specs=[vm, vm] + [hbm] * 7,
        out_specs=(vm, vm),
        scratch_shapes=[
            pltpu.VMEM((tok, half), BF),
            pltpu.VMEM((tok, width_q), BF),
            pltpu.VMEM((EXPERTS * SLOT, half), BF),
            pltpu.VMEM((EXPERTS * SLOT, half), BF),
            pltpu.VMEM((2, HOSTS, crows, half), BF),
            pltpu.VMEM((2 * half, 2 * ff), BF),
            pltpu.VMEM((2 * ff, half), BF),
            pltpu.VMEM((2, HOSTS, crows, ff), BF),
            pltpu.VMEM((HOSTS, crows, half), BF),
            pltpu.VMEM((2, 7, crows // 2, half), BF),
            pltpu.VMEM((EXPERTS * SLOT, half), BF),
            pltpu.VMEM((EXPERTS * SLOT, half), BF),
            pltpu.VMEM((tok, EXPERTS * SLOT), BF),
            pltpu.VMEM((tok, HEAD), F32),
            pltpu.VMEM((total, 2 * kvw), BF),
            pltpu.VMEM((groups, qrows, HEAD), BF),
            pltpu.VMEM((groups, qrows, HEAD), F32),
            pltpu.VMEM((groups, qrows, HEAD), F32),
            pltpu.VMEM((groups, qrows, HEAD), F32),
            dma((10,)),
            dma((4, EXPERTS)), dma((4, EXPERTS)),
            dma((2, 4)), dma((2, 4)),
            dma((2, 10)), dma((2, 10)),
            dma((17,)), dma((17,)),
            dma((HOSTS,)), dma((HOSTS,)),
            dma((44,)), dma((44,)),
            dma((2, 14)), dma((2, 14)),
            dma((2, EXPERTS)), dma((2, EXPERTS)),
        ],
        compiler_params=pltpu.CompilerParams(
            collective_id=0, has_side_effects=True, vmem_limit_bytes=60 * 1024 * 1024
        ),
    )(route_ids.reshape(1, tok), route_gain.reshape(1, tok), hidden, queries, keys, values, w_gate, w_up, w_down)


def solution(mesh):
    in_specs = (
        P("ctx", "tp"),
        P("ctx", "tp"),
        P("ctx", "tp"),
        P("ctx", "tp"),
        P("ctx", None),
        P("ctx"),
        P("ctx", None, "tp"),
        P("ctx", None, "tp"),
        P("ctx", None, "tp"),
    )
    out_specs = (P("ctx", "tp"), P("ctx", "tp"))
    return jax.shard_map(body, mesh=mesh, in_specs=in_specs, out_specs=out_specs, check_vma=False)
```

time: 125 us -> 116 us (0.928)
  Pallas kernels: 117 us -> 111 us
  local copies, waits for them, and re-layouts: 6.03 us -> 3.31 us
    pallas_call x1, Pallas kernels: 117 us -> 111 us  [body(): pl.pallas_call(kernel, name='layer', out_shape=(jax.ShapeDtypeStruct((tok...]
    unnamed x3 -> x2, local copies, waits for them, and re-layouts: 4.67 us -> 3.31 us
    broadcast_in_dim x1 -> x0, local copies, waits for them, and re-layouts: 1.36 us -> none  [body(): route_gain[:, None]]
where the time goes in v3:
time: 116 us; the launch traced here: 115 us
  Pallas kernels  111 us (96%)
  local copies, waits for them, and re-layouts  3.31 us (3%)
    pallas_call x1, Pallas kernels, body(): pl.pallas_call(kernel, name='layer', out_shape=(jax.ShapeDtypeStruct((tok...  111 us
    unnamed x2, local copies, waits for them, and re-layouts  3.31 us

profile of v3, /device:TPU:30, one launch (start us, length us, event | category | flops | bytes accessed | tf_op | source)
XLA Modules:
  0.0 114.6 jit_solution(5275189703438492681)
XLA Ops:
  0.6 110.6 %layer.1 = (bf16[64,1280]{1,0:T(8,128)(2,1)}, bf16[64,2560]{1,0:T(8,128)(2,1)}) custom-call(s32[1,64]{1,0:T(1,128)} %bitcast.2, f32[1,64]{1,0:T(1,128)} %bitcast.3, bf16[64,2560]{1,0:T(8,128)(2,1)} %hidden_ref.1, bf16[64,1280]{1,0:T(8,128)(2,1)} %q_ref.1, bf16[64,256]{1,0:T(8,128)(2,1)} %keys_ref.1, bf16[64,256]{1,0:T(8,128)(2,1)} %values_ref.1, ...), custom_call_target="tpu_custom_call" | custom-call | tf_op jit(solution)/shard_map/layer/pallas_call | solution.py:510
  111.3 1.6 %copy.13 = bf16[64,1280]{1,0:T(8,128)(2,1)} copy(bf16[64,1280]{1,0:T(8,128)(2,1)} %get-tuple-element.4) | data formatting | bytes 327680
  112.9 1.7 %copy.14 = bf16[64,2560]{1,0:T(8,128)(2,1)} copy(bf16[64,2560]{1,0:T(8,128)(2,1)} %get-tuple-element.5) | data formatting | bytes 655360

commit v4 on v3

--- a/solution.py
+++ b/solution.py
@@ -30,8 +30,8 @@
 
 def kernel(
     ids_ref, gain_ref, hidden_ref, q_ref, keys_ref, values_ref, wg_ref, wu_ref, wd_ref,
-    att_ref, mix_ref,
-    hid, qin, packed, a2a_in, rows_all, wgu, wd, inner_all, parts, rs_in, back_out, back_in, sel_ref, gain_col,
+    att_hbm, mix_hbm,
+    att_ref, mix_ref, hid, qin, packed, a2a_in, rows_all, wgu, wd, inner_all, parts, rs_in, back_out, back_in, sel_ref, gain_col,
     kv, qs, m_ref, l_ref, acc_ref,
     local_sem, a2a_s, a2a_r, kvz_s, kvz_r, zg_s, zg_r, px_s, px_r, in_s, in_r, kv_s, kv_r, rs_s, rs_r, bk_s, bk_r,
 ):
@@ -98,10 +98,13 @@
     sel = sel.astype(BF)
     local[0].wait()
     for c in range(0, half, quarter):
-        packed[:, c : c + quarter] = dot(sel, hid[:, c : c + quarter]).astype(BF)
+        packed[:, :, c : c + quarter] = dot(sel, hid[:, c : c + quarter]).reshape(EXPERTS, SLOT, quarter).astype(BF)
     m_ref[...] = jnp.full_like(m_ref, NEG)
     l_ref[...] = jnp.zeros_like(l_ref)
     acc_ref[...] = jnp.zeros_like(acc_ref)
+    unread = jnp.zeros((EXPERTS, SLOT - CAP, half), BF)
+    a2a_in[:, CAP:, :] = unread
+    back_in[:, CAP:, :] = unread
     local[1].wait()
     local[2].wait()
 
@@ -127,13 +130,13 @@
     kvz_go(0)
 
     def slot_rows(q):
-        return pl.ds(pl.multiple_of(q * SLOT, SLOT), SLOT)
+        return q, pl.ds(0, CAP)
 
     def a2a(i, c):
         q = plane_at(i)
         cols = pl.ds(c * quarter, quarter)
         return remote(
-            packed.at[slot_rows(q), cols], a2a_in.at[slot_rows(p), cols], a2a_s.at[c, i], a2a_r.at[c, i], dev_plane(q)
+            packed.at[(*slot_rows(q), cols)], a2a_in.at[(*slot_rows(p), cols)], a2a_s.at[c, i], a2a_r.at[c, i], dev_plane(q)
         )
 
     keep = pltpu.make_async_copy(packed.at[slot_rows(p)], a2a_in.at[slot_rows(p)], local_sem.at[7])
@@ -260,10 +263,10 @@
     for c in range(4):
         cols = pl.ds(c * quarter, quarter)
         for i in range(1, EXPERTS):
-            ref = a2a_in.at[slot_rows(plane_at(EXPERTS - i)), cols]
+            ref = a2a_in.at[(*slot_rows(plane_at(EXPERTS - i)), cols)]
             remote(ref, ref, a2a_s.at[c, i], a2a_r.at[c, i], dev_plane(plane_at(i))).wait_recv()
         rows_all[core, z, :, c * quarter : (c + 1) * quarter] = dot(
-            dense, a2a_in[:, c * quarter : (c + 1) * quarter]
+            dense, a2a_in[:, :, c * quarter : (c + 1) * quarter].astype(F32).reshape(EXPERTS * SLOT, quarter).astype(BF)
         ).astype(BF)
         if c in (0, 1):
             kvz_wait(c + 1)
@@ -425,7 +428,7 @@
         q = plane_at(i)
         cols = pl.ds(c * chalf, chalf)
         return remote(
-            back_out.at[slot_rows(q), cols], back_in.at[slot_rows(p), cols], bk_s.at[c, i], bk_r.at[c, i], dev_plane(q)
+            back_out.at[(*slot_rows(q), cols)], back_in.at[(*slot_rows(p), cols)], bk_s.at[c, i], bk_r.at[c, i], dev_plane(q)
         )
 
     def finish(c):
@@ -438,10 +441,12 @@
             for direction in (0, 1):
                 total = total + rs_slot(direction, direction ^ h, 1, c)[...].astype(F32)
             n = EXPERTS * SLOT // 2
-            back_out[h * n : (h + 1) * n, cols] = dot(spread, total.astype(BF)).astype(BF)
+            back_out[h * (EXPERTS // 2) : (h + 1) * (EXPERTS // 2), :, cols] = (
+                dot(spread, total.astype(BF)).reshape(EXPERTS // 2, SLOT, chalf).astype(BF)
+            )
         stay = pltpu.make_async_copy(
-            back_out.at[slot_rows(p), pl.ds(c * chalf, chalf)],
-            back_in.at[slot_rows(p), pl.ds(c * chalf, chalf)],
+            back_out.at[(*slot_rows(p), pl.ds(c * chalf, chalf))],
+            back_in.at[(*slot_rows(p), pl.ds(c * chalf, chalf))],
             local_sem.at[8 + c],
         )
         stay.start()
@@ -451,11 +456,13 @@
 
     def mix(c, stay):
         for i in range(1, EXPERTS):
-            ref = back_in.at[slot_rows(plane_at(EXPERTS - i)), pl.ds(c * chalf, chalf)]
+            ref = back_in.at[(*slot_rows(plane_at(EXPERTS - i)), pl.ds(c * chalf, chalf))]
             remote(ref, ref, bk_s.at[c, i], bk_r.at[c, i], dev_plane(plane_at(i))).wait_recv()
         stay.wait()
         for b in range(c * chalf, (c + 1) * chalf, quarter):
-            own = dot(sel_ref[...], back_in[:, b : b + quarter])
+            own = dot(
+                sel_ref[...], back_in[:, :, b : b + quarter].astype(F32).reshape(EXPERTS * SLOT, quarter).astype(BF)
+            )
             for t in range(0, quarter, HEAD):
                 mix_ref[:, b + t : b + t + HEAD] = (own[:, t : t + HEAD] * gain_col[...]).astype(BF)
 
@@ -466,6 +473,8 @@
             i = g * heads + h
             att_ref[:, i * HEAD : (i + 1) * HEAD] = out[h * tok : (h + 1) * tok].astype(BF)
     second = finish(1)
+    att_out = pltpu.make_async_copy(att_ref, att_hbm, local_sem.at[10])
+    att_out.start()
 
     for c in range(4):
         for i in range(1, EXPERTS):
@@ -490,10 +499,26 @@
             kv_copy(*c).wait_send()
 
     mix(0, first)
+    mix_out = [
+        pltpu.make_async_copy(
+            mix_ref.at[:, pl.ds(c * chalf, chalf)], mix_hbm.at[:, pl.ds(c * chalf, chalf)], local_sem.at[11 + c]
+        )
+        for c in (0, 1)
+    ]
+    mix_out[0].start()
     mix(1, second)
+    mix_out[1].start()
+    att_out.wait()
+    mix_out[0].wait()
+    mix_out[1].wait()
     for c in (0, 1):
         for i in range(1, EXPERTS):
             back(i, c).wait_send()
+
+
+def closing(a_ref, b_ref, a_out, b_out):
+    a_out[...] = a_ref[...]
+    b_out[...] = b_ref[...]
 
 
 def body(queries, keys, values, hidden, route_ids, route_gain, w_gate, w_up, w_down):
@@ -507,7 +532,7 @@
     vm = pl.BlockSpec(memory_space=pltpu.VMEM)
     hbm = pl.BlockSpec(memory_space=pl.ANY)
     dma = pltpu.SemaphoreType.DMA
-    return pl.pallas_call(
+    attended, mixed = pl.pallas_call(
         kernel,
         name="layer",
         out_shape=(
@@ -515,20 +540,22 @@
             jax.ShapeDtypeStruct((tok, half), BF),
         ),
         in_specs=[vm, vm] + [hbm] * 7,
-        out_specs=(vm, vm),
+        out_specs=(hbm, hbm),
         scratch_shapes=[
+            pltpu.VMEM((tok, width_q), BF),
+            pltpu.VMEM((tok, half), BF),
             pltpu.VMEM((tok, half), BF),
             pltpu.VMEM((tok, width_q), BF),
-            pltpu.VMEM((EXPERTS * SLOT, half), BF),
-            pltpu.VMEM((EXPERTS * SLOT, half), BF),
+            pltpu.VMEM((EXPERTS, SLOT, half), BF),
+            pltpu.VMEM((EXPERTS, SLOT, half), BF),
             pltpu.VMEM((2, HOSTS, crows, half), BF),
             pltpu.VMEM((2 * half, 2 * ff), BF),
             pltpu.VMEM((2 * ff, half), BF),
             pltpu.VMEM((2, HOSTS, crows, ff), BF),
             pltpu.VMEM((HOSTS, crows, half), BF),
             pltpu.VMEM((2, 7, crows // 2, half), BF),
-            pltpu.VMEM((EXPERTS * SLOT, half), BF),
-            pltpu.VMEM((EXPERTS * SLOT, half), BF),
+            pltpu.VMEM((EXPERTS, SLOT, half), BF),
+            pltpu.VMEM((EXPERTS, SLOT, half), BF),
             pltpu.VMEM((tok, EXPERTS * SLOT), BF),
             pltpu.VMEM((tok, HEAD), F32),
             pltpu.VMEM((total, 2 * kvw), BF),
@@ -536,7 +563,7 @@
             pltpu.VMEM((groups, qrows, HEAD), F32),
             pltpu.VMEM((groups, qrows, HEAD), F32),
             pltpu.VMEM((groups, qrows, HEAD), F32),
-            dma((10,)),
+            dma((13,)),
             dma((4, EXPERTS)), dma((4, EXPERTS)),
             dma((2, 4)), dma((2, 4)),
             dma((2, 10)), dma((2, 10)),
@@ -550,6 +577,13 @@
             collective_id=0, has_side_effects=True, vmem_limit_bytes=60 * 1024 * 1024
         ),
     )(route_ids.reshape(1, tok), route_gain.reshape(1, tok), hidden, queries, keys, values, w_gate, w_up, w_down)
+    return pl.pallas_call(
+        closing,
+        name="closing",
+        out_shape=(jax.ShapeDtypeStruct((tok, width_q), BF), jax.ShapeDtypeStruct((tok, half), BF)),
+        in_specs=[vm, vm],
+        out_specs=(vm, vm),
+    )(attended, mixed)
 
 
 def solution(mesh):

time: 116 us -> 114 us (0.983)
  local copies, waits for them, and re-layouts: 3.31 us -> 0 us
    unnamed x2 -> x0, local copies, waits for them, and re-layouts: 3.31 us -> none
    pallas_call x0 -> x1, Pallas kernels: none -> 1.85 us  [body(): pl.pallas_call(closing, name='closing', out_shape=(jax.ShapeDtypeStruct((...]
where the time goes in v4:
time: 114 us; the launch traced here: 113 us
  Pallas kernels  112 us (98%)
    pallas_call x1, Pallas kernels, body(): pl.pallas_call(kernel, name='layer', out_shape=(jax.ShapeDtypeStruct((tok...  110 us

profile of v4, /device:TPU:30, one launch (start us, length us, event | category | flops | bytes accessed | tf_op | source)
XLA Modules:
  0.0 112.7 jit_solution(7227543116590379237)
XLA Ops:
  0.6 110.3 %layer.1 = (bf16[64,1280]{1,0:T(8,128)(2,1)}, bf16[64,2560]{1,0:T(8,128)(2,1)}) custom-call(s32[1,64]{1,0:T(1,128)} %bitcast.2, f32[1,64]{1,0:T(1,128)} %bitcast.3, bf16[64,2560]{1,0:T(8,128)(2,1)} %hidden_ref.1, bf16[64,1280]{1,0:T(8,128)(2,1)} %q_ref.1, bf16[64,256]{1,0:T(8,128)(2,1)} %keys_ref.1, bf16[64,256]{1,0:T(8,128)(2,1)} %values_ref.1, ...), custom_call_target="tpu_custom_call" | custom-call | tf_op jit(solution)/shard_map/layer/pallas_call | solution.py:535
  110.9 1.9 %closing.1 = (bf16[64,1280]{1,0:T(8,128)(2,1)}, bf16[64,2560]{1,0:T(8,128)(2,1)}) custom-call(bf16[64,1280]{1,0:T(8,128)(2,1)} %get-tuple-element.4.a_ref, bf16[64,2560]{1,0:T(8,128)(2,1)} %get-tuple-element.5.b_ref), custom_call_target="tpu_custom_call" | custom-call | tf_op jit(solution)/shard_map/closing/pallas_call | solution.py:580

commit v5 on v4

--- a/solution.py
+++ b/solution.py
@@ -49,6 +49,7 @@
     heads = q_ref.shape[1] // HEAD // groups
     width = wg_ref.shape[2]
     chalf, quarter = half // 2, half // 4
+    group = ((0, 1536), (1536, half - 1536))
 
     def zat(d):
         return lax.rem(z + d + HOSTS, HOSTS)
@@ -57,7 +58,15 @@
         return {"ctx": p * HOSTS + zat(d), "tp": core}
 
     def plane_at(i):
-        return lax.rem(p + i, EXPERTS)
+        return lax.rem(px + i // SIDE, SIDE) * SIDE + lax.rem(py + i % SIDE, SIDE)
+
+    def plane_from(i):
+        return lax.rem(px + SIDE - i // SIDE, SIDE) * SIDE + lax.rem(py + SIDE - i % SIDE, SIDE)
+
+    def hops(i):
+        return min(i // SIDE, SIDE - i // SIDE) + min(i % SIDE, SIDE - i % SIDE)
+
+    shifts = sorted(range(1, EXPERTS), key=lambda i: -hops(i))
 
     def dev_plane(q):
         return {"ctx": q * HOSTS + z, "tp": core}
@@ -71,7 +80,7 @@
         )
 
     barrier = pltpu.get_barrier_semaphore()
-    greeted = [dev_plane(plane_at(i)) for i in range(1, EXPERTS)] + [dev_z(1), dev_z(-1), partner]
+    greeted = [dev_plane(plane_at(i)) for i in shifts] + [dev_z(1), dev_z(-1), partner]
     for device in greeted:
         pl.semaphore_signal(barrier, inc=1, device_id=device, device_id_type=MESH)
 
@@ -142,7 +151,7 @@
     keep = pltpu.make_async_copy(packed.at[slot_rows(p)], a2a_in.at[slot_rows(p)], local_sem.at[7])
     keep.start()
     for c in range(4):
-        for i in range(1, EXPERTS):
+        for i in shifts:
             a2a(i, c).start()
 
     def shifted(part, d1, d2):
@@ -262,8 +271,8 @@
     keep.wait()
     for c in range(4):
         cols = pl.ds(c * quarter, quarter)
-        for i in range(1, EXPERTS):
-            ref = a2a_in.at[(*slot_rows(plane_at(EXPERTS - i)), cols)]
+        for i in shifts:
+            ref = a2a_in.at[(*slot_rows(plane_from(i)), cols)]
             remote(ref, ref, a2a_s.at[c, i], a2a_r.at[c, i], dev_plane(plane_at(i))).wait_recv()
         rows_all[core, z, :, c * quarter : (c + 1) * quarter] = dot(
             dense, a2a_in[:, :, c * quarter : (c + 1) * quarter].astype(F32).reshape(EXPERTS * SLOT, quarter).astype(BF)
@@ -311,8 +320,6 @@
     arrive(3)
     pair(inner_wait, 1)
     pair(down, 1)
-    kv_wait("s2a")
-    kv_start("f2a")
 
     arrive(4)
     ready(2)
@@ -322,6 +329,8 @@
     arrive(5)
     pair(inner_wait, 2)
     pair(down, 2)
+    kv_wait("s2a")
+    kv_start("f2a")
     ready(3)
     pair(gate_up, 3)
     pair(lambda zs: inner_copy(zs).start(), 3)
@@ -330,10 +339,10 @@
         return pl.ds((direction ^ chain) * hrows, hrows)
 
     def rs_part(direction, chain, t, c):
-        return parts.at[zat(signs[direction] * t), rs_rows(direction, chain), pl.ds(c * chalf, chalf)]
+        return parts.at[zat(signs[direction] * t), rs_rows(direction, chain), pl.ds(*group[c])]
 
     def rs_slot(direction, chain, t, c):
-        return rs_in.at[direction, chain * 4 + t - 1, :, pl.ds(c * chalf, chalf)]
+        return rs_in.at[direction, chain * 4 + t - 1, :, pl.ds(*group[c])]
 
     def rs(direction, chain, t, c):
         n = (chain * 4 + t - 1) * 2 + c
@@ -426,7 +435,7 @@
 
     def back(i, c):
         q = plane_at(i)
-        cols = pl.ds(c * chalf, chalf)
+        cols = pl.ds(*group[c])
         return remote(
             back_out.at[(*slot_rows(q), cols)], back_in.at[(*slot_rows(p), cols)], bk_s.at[c, i], bk_r.at[c, i], dev_plane(q)
         )
@@ -435,35 +444,35 @@
         for direction in (0, 1):
             rs(direction, 1, 1, c).wait_recv()
             rs(direction, 0, 1, c).wait_recv()
-        cols = slice(c * chalf, (c + 1) * chalf)
+        cols = slice(group[c][0], sum(group[c]))
         for h in (0, 1):
             total = parts[z, h * hrows : (h + 1) * hrows, cols].astype(F32)
             for direction in (0, 1):
                 total = total + rs_slot(direction, direction ^ h, 1, c)[...].astype(F32)
             n = EXPERTS * SLOT // 2
             back_out[h * (EXPERTS // 2) : (h + 1) * (EXPERTS // 2), :, cols] = (
-                dot(spread, total.astype(BF)).reshape(EXPERTS // 2, SLOT, chalf).astype(BF)
+                dot(spread, total.astype(BF)).reshape(EXPERTS // 2, SLOT, group[c][1]).astype(BF)
             )
         stay = pltpu.make_async_copy(
-            back_out.at[(*slot_rows(p), pl.ds(c * chalf, chalf))],
-            back_in.at[(*slot_rows(p), pl.ds(c * chalf, chalf))],
+            back_out.at[(*slot_rows(p), pl.ds(*group[c]))],
+            back_in.at[(*slot_rows(p), pl.ds(*group[c]))],
             local_sem.at[8 + c],
         )
         stay.start()
-        for i in range(1, EXPERTS):
+        for i in shifts:
             back(i, c).start()
         return stay
 
     def mix(c, stay):
-        for i in range(1, EXPERTS):
-            ref = back_in.at[(*slot_rows(plane_at(EXPERTS - i)), pl.ds(c * chalf, chalf))]
+        for i in shifts:
+            ref = back_in.at[(*slot_rows(plane_from(i)), pl.ds(*group[c]))]
             remote(ref, ref, bk_s.at[c, i], bk_r.at[c, i], dev_plane(plane_at(i))).wait_recv()
         stay.wait()
-        for b in range(c * chalf, (c + 1) * chalf, quarter):
+        for b in range(group[c][0], sum(group[c]), 512):
             own = dot(
-                sel_ref[...], back_in[:, :, b : b + quarter].astype(F32).reshape(EXPERTS * SLOT, quarter).astype(BF)
+                sel_ref[...], back_in[:, :, b : b + 512].astype(F32).reshape(EXPERTS * SLOT, 512).astype(BF)
             )
-            for t in range(0, quarter, HEAD):
+            for t in range(0, 512, HEAD):
                 mix_ref[:, b + t : b + t + HEAD] = (own[:, t : t + HEAD] * gain_col[...]).astype(BF)
 
     first = finish(0)
@@ -477,7 +486,7 @@
     att_out.start()
 
     for c in range(4):
-        for i in range(1, EXPERTS):
+        for i in shifts:
             a2a(i, c).wait_send()
     for direction in (0, 1):
         for n in range(4):
@@ -501,7 +510,7 @@
     mix(0, first)
     mix_out = [
         pltpu.make_async_copy(
-            mix_ref.at[:, pl.ds(c * chalf, chalf)], mix_hbm.at[:, pl.ds(c * chalf, chalf)], local_sem.at[11 + c]
+            mix_ref.at[:, pl.ds(*group[c])], mix_hbm.at[:, pl.ds(*group[c])], local_sem.at[11 + c]
         )
         for c in (0, 1)
     ]
@@ -512,7 +521,7 @@
     mix_out[0].wait()
     mix_out[1].wait()
     for c in (0, 1):
-        for i in range(1, EXPERTS):
+        for i in shifts:
             back(i, c).wait_send()
 
 

time: 114 us -> 111 us (0.974)
  Pallas kernels: 112 us -> 109 us
    pallas_call x1, Pallas kernels: 110 us -> 108 us  [body(): pl.pallas_call(kernel, name='layer', out_shape=(jax.ShapeDtypeStruct((tok...]
where the time goes in v5:
time: 111 us; the launch traced here: 110 us
  Pallas kernels  109 us (98%)
    pallas_call x1, Pallas kernels, body(): pl.pallas_call(kernel, name='layer', out_shape=(jax.ShapeDtypeStruct((tok...  108 us

profile of v5, /device:TPU:30, one launch (start us, length us, event | category | flops | bytes accessed | tf_op | source)
XLA Modules:
  0.0 110.0 jit_solution(11486909867983397737)
XLA Ops:
  0.6 107.5 %layer.1 = (bf16[64,1280]{1,0:T(8,128)(2,1)}, bf16[64,2560]{1,0:T(8,128)(2,1)}) custom-call(s32[1,64]{1,0:T(1,128)} %bitcast.2, f32[1,64]{1,0:T(1,128)} %bitcast.3, bf16[64,2560]{1,0:T(8,128)(2,1)} %hidden_ref.1, bf16[64,1280]{1,0:T(8,128)(2,1)} %q_ref.1, bf16[64,256]{1,0:T(8,128)(2,1)} %keys_ref.1, bf16[64,256]{1,0:T(8,128)(2,1)} %values_ref.1, ...), custom_call_target="tpu_custom_call" | custom-call | tf_op jit(solution)/shard_map/layer/pallas_call | solution.py:544
  108.2 1.9 %closing.1 = (bf16[64,1280]{1,0:T(8,128)(2,1)}, bf16[64,2560]{1,0:T(8,128)(2,1)}) custom-call(bf16[64,1280]{1,0:T(8,128)(2,1)} %get-tuple-element.4.a_ref, bf16[64,2560]{1,0:T(8,128)(2,1)} %get-tuple-element.5.b_ref), custom_call_target="tpu_custom_call" | custom-call | tf_op jit(solution)/shard_map/closing/pallas_call | solution.py:589
